TPU v7x, 256 devices: a whole 4x4x8 slice. The times are simulated.
256 devices in a mesh: section: 8 (over z), dp: 32 (over x, y, core).
Axes of the slice: x: 4, y: 4, z: 8, core: 2. Of those that a mesh axis runs over, the one named last changes fastest.
Arguments:
- entry: bfloat16 [6144, 3584], P('dp'), may hold values from -6 to 6
- norm_gain: float32 [8, 3584], P('section'), may hold values from 0.5 to 1.5
- w_qkv: bfloat16 [8, 3584, 1152], P('section', 'dp'), may hold values from -0.09375 to 0.09375
- w_out: bfloat16 [8, 896, 3584], P('section', 'dp'), may hold values from -0.1875 to 0.1875
- final_gain: float32 [3584], replicated, may hold values from 0.5 to 1.5
- lengths: int32 [128], P('dp'), may hold values from 24 to 48
- positive: int32 [64], P('dp'), may hold values from 0 to 63, each once
Outputs:
- section_grads: bfloat16 [8, 6144, 3584], P('section', 'dp')
Inputs may be any that keep to these rules, and one draw needn't show every extreme that they name: lengths[j] is the count of tokens of sequence j; its last token is pooled. Each document index is the positive of exactly one query.
All inputs are finite; a program needn't handle non-finite values.
Results may differ from a plain program's by a relative error of at most 0.022.
Values may be sent and summed in bfloat16 or wider, within the bound.
A program may use at most 192 MiB of HBM per device.

v0:
```python
import jax
import jax.numpy as jnp
from jax import lax
from jax.sharding import Mesh
from jax.sharding import PartitionSpec as P

HEAD_DIM = 64
GROUP_HEADS = 7
KV_GROUPS = 2
DP = ("dp_0", "dp_1", "dp_2")


rope_base = 1000000.0
norm_eps = 1e-06
sharpness_divisor = 0.05
objective_coefficient = 256.0


def laid_out(pieces, dim):
    pieces = jnp.moveaxis(pieces, 0, dim)
    lengths = pieces.shape
    return pieces.reshape(*lengths[:dim], lengths[dim] * lengths[dim + 1], *lengths[dim + 2 :])


def one_gather(arrays, axis, dims):
    vector = jnp.concatenate([a.reshape(-1) for a in arrays])
    lines, at, gathered = (lax.all_gather(vector, axis), 0, [])
    for a, dim in zip(arrays, dims):
        pieces = lines[:, at : at + a.size].reshape(-1, *a.shape)
        gathered.append(laid_out(pieces, dim))
        at += a.size
    return tuple(gathered)


def shifted(value, axis, steps):
    count = lax.axis_size(axis)
    first, last = (max(0, -steps), min(count, count - steps))
    return lax.ppermute(value, axis, [(source, source + steps) for source in range(first, last)])


def copy_for_each(shard, axis):
    copies = jnp.broadcast_to(shard, (lax.axis_size(axis), *shard.shape))
    return lax.all_to_all(copies, axis, split_axis=0, concat_axis=0, tiled=True)


def gathered_copies(shard, axis, dim):
    return laid_out(copy_for_each(shard, axis), dim)


def gathered_by_axis(shard, axes, dim):
    if not axes:
        return shard
    nearer = lax.all_gather(shard, axes[-1], axis=dim, tiled=True)
    return gathered_by_axis(nearer, axes[:-1], dim)


def rotary(values, positions):
    half_dim = values.shape[-1] // 2
    frequency = rope_base ** (-jnp.arange(half_dim, dtype=jnp.float32) * (2.0 / values.shape[-1]))
    angles = positions.astype(jnp.float32)[:, None] * frequency[None, :]
    cosine = jnp.cos(angles)[:, None, :]
    sine_part = jnp.sin(angles)[:, None, :]
    first_half = values[..., :half_dim]
    second_half = values[..., half_dim:]
    return jnp.concatenate(
        [
            first_half * cosine - second_half * sine_part,
            second_half * cosine + first_half * sine_part,
        ],
        axis=-1,
    )


def rms_scale(values, gain_row):
    return (
        values * lax.rsqrt(jnp.mean(values * values, axis=-1, keepdims=True) + norm_eps) * gain_row
    )


def attention_layer(hidden, seq_lengths, gain_row, weight_qkv, weight_out):
    row_count, row_width = hidden.shape
    seq_count = seq_lengths.shape[0]
    length = row_count // seq_count
    q_width = weight_out.shape[0]
    kv_width = KV_GROUPS * HEAD_DIM
    wide_in = hidden.astype(jnp.float32)
    normed = rms_scale(wide_in, gain_row).astype(jnp.bfloat16)
    projected = jnp.dot(normed, weight_qkv, preferred_element_type=jnp.float32)
    positions = jnp.arange(length, dtype=jnp.int32)
    query_rot = rotary(
        projected[:, :q_width].reshape(seq_count, length, KV_GROUPS * GROUP_HEADS, HEAD_DIM),
        positions,
    ).astype(jnp.bfloat16)
    key_rot = rotary(
        projected[:, q_width : q_width + kv_width].reshape(seq_count, length, KV_GROUPS, HEAD_DIM),
        positions,
    ).astype(jnp.bfloat16)
    value_rows = (
        projected[:, q_width + kv_width :]
        .reshape(seq_count, length, KV_GROUPS, HEAD_DIM)
        .astype(jnp.bfloat16)
    )
    query_grid = query_rot.reshape(seq_count, length, KV_GROUPS, GROUP_HEADS, HEAD_DIM)
    scores = jnp.einsum(
        "sqgzd,skgd->sgzqk", query_grid.astype(jnp.float32), key_rot.astype(jnp.float32)
    ) * HEAD_DIM ** (-0.5)
    key_live = positions[None, :] < seq_lengths[:, None]
    weights = jnp.where(key_live[:, None, None, None, :], jnp.exp(scores), 0.0)
    prob_low = (weights / jnp.sum(weights, axis=-1, keepdims=True)).astype(jnp.bfloat16)
    context = jnp.einsum(
        "sgzqk,skgd->sqgzd", prob_low.astype(jnp.float32), value_rows.astype(jnp.float32)
    ).astype(jnp.bfloat16)
    branch = jnp.dot(
        context.reshape(row_count, q_width), weight_out, preferred_element_type=jnp.float32
    )
    return (wide_in + branch).astype(jnp.bfloat16)


def embed_rows(rows_in, final_gain):
    pooled = rms_scale(rows_in.astype(jnp.float32), final_gain)
    return pooled * lax.rsqrt(jnp.sum(pooled * pooled, axis=-1, keepdims=True))


def pair_terms(question_representation, passage_representation, positive):
    match_raw_scores = jnp.dot(
        question_representation, passage_representation.T, preferred_element_type=jnp.float32
    ) * (1.0 / sharpness_divisor)
    weights = jnp.exp(match_raw_scores)
    normalized_exponential_odds = weights / jnp.sum(weights, axis=-1, keepdims=True)
    correct_target_column = (
        positive[:, None] == jnp.arange(passage_representation.shape[0], dtype=jnp.int32)[None, :]
    ).astype(jnp.float32)
    return (normalized_exponential_odds - correct_target_column) * (
        objective_coefficient / sharpness_divisor
    )


def per_device(entry, norm_gain, w_qkv, w_out, final_gain, lengths, positive):
    section_id = lax.axis_index("section")
    section_count = lax.axis_size("section")
    row_width = entry.shape[1]
    micro_count = positive.shape[0]
    rows_micro = entry.shape[0] // micro_count
    length = rows_micro // 2
    full_qkv, full_out = one_gather((w_qkv, w_out), DP, (1, 1))
    full_qkv = full_qkv[0]
    full_out = full_out[0]
    gain_row = norm_gain[0]
    tick_count = micro_count + section_count - 1

    def apply_layer(values, seq_lengths):
        return attention_layer(values, seq_lengths, gain_row, full_qkv, full_out)

    def pieces(micro_id):
        slot_id = jnp.clip(micro_id, 0, micro_count - 1)
        seq_lengths = lax.dynamic_slice_in_dim(lengths, slot_id * 2, 2, 0)
        return (slot_id, seq_lengths)

    zero_stack = jnp.zeros((micro_count, rows_micro, row_width), jnp.bfloat16)
    zero_block = jnp.zeros((rows_micro, row_width), jnp.bfloat16)

    def forward_tick(tick_id, state_in):
        inbox_buf, stash_buf, final_out = state_in
        micro_id = tick_id - section_id
        is_live = jnp.logical_and(micro_id >= 0, micro_id < micro_count)
        slot_id, seq_lengths = pieces(micro_id)
        fresh_rows = lax.dynamic_slice_in_dim(entry, slot_id * rows_micro, rows_micro, 0)
        current = jnp.where(section_id == 0, fresh_rows, inbox_buf)
        result = lax.cond(
            is_live, lambda values: apply_layer(values, seq_lengths), lambda values: values, current
        )
        stash_buf = lax.dynamic_update_index_in_dim(
            stash_buf, jnp.where(is_live, current, stash_buf[slot_id]), slot_id, 0
        )
        keep_top = jnp.logical_and(is_live, section_id == section_count - 1)
        final_out = lax.dynamic_update_index_in_dim(
            final_out, jnp.where(keep_top, result, final_out[slot_id]), slot_id, 0
        )
        inbox_buf = shifted(result, "section", 1)
        return (inbox_buf, stash_buf, final_out)

    _, stash_buf, final_out = lax.fori_loop(
        0, tick_count, forward_tick, (zero_block, zero_stack, zero_stack)
    )
    seq_grid = final_out.reshape(micro_count * 2, length, row_width)
    last_rows = jnp.take_along_axis(seq_grid, (lengths - 1)[:, None, None], axis=1)[:, 0]
    embedding, back_embed = jax.vjp(lambda rows_in: embed_rows(rows_in, final_gain), last_rows)
    emb_low = embedding.astype(jnp.bfloat16)
    question_representation = emb_low[0::2]
    passage_representation = emb_low[1::2]
    replica = lax.axis_index(DP)
    both_embed = gathered_copies(
        jnp.stack([question_representation, passage_representation]), DP, 1
    )
    pair_all = gathered_by_axis(positive, DP, 0)
    pair_coef = pair_terms(both_embed[0], both_embed[1], pair_all)
    grad_query_all = jnp.dot(pair_coef, both_embed[1].astype(jnp.float32))
    grad_doc_all = jnp.dot(pair_coef.T, both_embed[0].astype(jnp.float32))
    grad_query = lax.dynamic_slice_in_dim(grad_query_all, replica * micro_count, micro_count, 0)
    grad_doc = lax.dynamic_slice_in_dim(grad_doc_all, replica * micro_count, micro_count, 0)
    grad_emb = jnp.stack([grad_query, grad_doc], axis=1).reshape(micro_count * 2, row_width)
    grad_last = back_embed(grad_emb)[0]
    slot_hit = jnp.arange(length, dtype=jnp.int32)[None, :] == (lengths - 1)[:, None]
    seed_grad = jnp.where(slot_hit[:, :, None], grad_last[:, None, :], 0).reshape(
        micro_count, rows_micro, row_width
    )

    def backward_tick(tick_id, state_in):
        inbox_buf, grad_buf = state_in
        micro_id = tick_id - (section_count - 1 - section_id)
        is_live = jnp.logical_and(micro_id >= 0, micro_id < micro_count)
        slot_id, seq_lengths = pieces(micro_id)
        upstream = jnp.where(section_id == section_count - 1, seed_grad[slot_id], inbox_buf)

        def pull_back(operand):
            saved_rows, cotangent = operand
            _, back_layer = jax.vjp(lambda values: apply_layer(values, seq_lengths), saved_rows)
            return back_layer(cotangent)[0]

        downstream = lax.cond(
            is_live, pull_back, lambda operand: operand[1], (stash_buf[slot_id], upstream)
        )
        grad_buf = lax.dynamic_update_index_in_dim(
            grad_buf, jnp.where(is_live, downstream, grad_buf[slot_id]), slot_id, 0
        )
        inbox_buf = shifted(downstream, "section", -1)
        return (inbox_buf, grad_buf)

    _, grad_buf = lax.fori_loop(0, tick_count, backward_tick, (zero_block, zero_stack))
    return grad_buf.reshape(1, micro_count * rows_micro, row_width)


def solution(mesh):
    finer = Mesh(
        mesh.devices.reshape(mesh.shape["section"], 4, 4, 2), ("section", "dp_0", "dp_1", "dp_2")
    )
    in_specs = (
        P(DP, None),
        P("section", None),
        P("section", DP, None),
        P("section", DP, None),
        P(),
        P(DP),
        P(DP),
    )
    out_specs = P("section", DP, None)
    return jax.shard_map(
        per_device, mesh=finer, in_specs=in_specs, out_specs=out_specs, check_vma=False
    )
```

profile of v0, /device:TPU:1, one launch (start us, length us, event | category | flops | bytes accessed | tf_op | source)
XLA Modules:
  0.0 959.0 jit_solution(15289980668878995511)
XLA Ops:
  11.2 75.7 %all-gather.3.cloned.1.call-done = bf16[7340032]{0:T(1024)(128)(2,1)} async-done(((bf16[229376]{0:T(1024)(128)(2,1)}), bf16[7340032]{0:T(1024)(128)(2,1)}) %all-gather.3.cloned.1.call-update) | async-done | bytes 14680080 | tf_op jit(solution)/shard_map/all_gather | solution.py:27
  86.9 13.2 %reshape.548 = bf16[32,229376]{1,0:T(8,128)(2,1)} reshape(bf16[7340032]{0:T(1024)(128)(2,1)} %all-gather.3.cloned.1.call-done) | data formatting | bytes 29360128 | tf_op jit(solution)/shard_map/all_gather | solution.py:27
  100.1 7.2 slice.116
  107.2 5.9 slice.117
  113.2 8.8 squeeze_reshape_transpose_reshape.6
  122.0 12.2 %squeeze_reshape_transpose_reshape.7 = bf16[896,3584]{1,0:T(8,128)(2,1)} reshape(bf16[32,100352]{1,0:T(8,128)(2,1)} %slice.117) | data formatting | bytes 12845056 | tf_op jit(solution)/shard_map/squeeze;reshape;transpose;reshape | solution.py:147
  135.5 256.3 %while.35 = (s32[]{:T(128)}, bf16[96,3584]{1,0:T(8,128)(2,1)S(1)}, bf16[2,96,3584]{2,1,0:T(8,128)(2,1)S(1)}, bf16[2,96,3584]{2,1,0:T(8,128)(2,1)}, s32[]{:T(128)...) while((s32[]{:T(128)}, bf16[96,3584]{1,0:T(8,128)(2,1)S(1)}, ...), condition=%wide.region_5.6_spmd, body=%wide.region_0.5_spmd.sunk | while | flops 1431407872 | bytes 44450632 | solution.py:182
  135.8 1.4 bitcast_dynamic-update-slice_fusion.6
  137.3 17.4 %conditional.4 = (bf16[96,3584]{1,0:T(8,128)(2,1)S(1)}) conditional(s32[]{:T(128)} %convert_element_type.382, bf16[96,3584]{1,0:T(8,128)(2,1)S(1)} %get-tuple-element.840, (bf16[96,3584]{1,0:T(8,128)(2,1)S(1)}, f32[1,3584]{1,0:T(1,128)}, bf16[3584,1152]{1,0:T(8,128)(2,1)}, s32[]{:T(128)}, s32[4]{0:T(128)}, ...), branch_computations={%region_1.1_spmd, %region_2.4_spmd} | conditional | flops 1430375680 | bytes 22430102 | solution.py:169
  138.3 4.9 fusion.8
  148.6 1.6 fusion.7
  150.6 4.1 fusion
  157.7 13.0 %collective-permute-done = bf16[96,3584]{1,0:T(8,128)(2,1)S(1)} collective-permute-done((bf16[96,3584]{1,0:T(8,128)(2,1)S(1)}, bf16[96,3584]{1,0:T(8,128)(2,1)S(1)}, u32[]{:S(2)}, u32[]{:S(2)}) %collective-permute-start) | collective-permute-done | bytes 688160 | tf_op jit(solution)/shard_map/while/body/eval_jaxpr/ppermute | solution.py:38
  172.3 17.4 %conditional.4 = (bf16[96,3584]{1,0:T(8,128)(2,1)S(1)}) conditional(s32[]{:T(128)} %convert_element_type.382, bf16[96,3584]{1,0:T(8,128)(2,1)S(1)} %get-tuple-element.840, (bf16[96,3584]{1,0:T(8,128)(2,1)S(1)}, f32[1,3584]{1,0:T(1,128)}, bf16[3584,1152]{1,0:T(8,128)(2,1)}, s32[]{:T(128)}, s32[4]{0:T(128)}, ...), branch_computations={%region_1.1_spmd, %region_2.4_spmd} | conditional | flops 1430375680 | bytes 22430102 | solution.py:169
  173.3 4.9 fusion.8
  183.5 1.6 fusion.7
  185.6 4.1 fusion
  189.7 4.1 collective-permute-start
  195.6 12.1 %collective-permute-done = bf16[96,3584]{1,0:T(8,128)(2,1)S(1)} collective-permute-done((bf16[96,3584]{1,0:T(8,128)(2,1)S(1)}, bf16[96,3584]{1,0:T(8,128)(2,1)S(1)}, u32[]{:S(2)}, u32[]{:S(2)}) %collective-permute-start) | collective-permute-done | bytes 688160 | tf_op jit(solution)/shard_map/while/body/eval_jaxpr/ppermute | solution.py:38
  209.2 21.5 %collective-permute-start = (bf16[96,3584]{1,0:T(8,128)(2,1)S(1)}, bf16[96,3584]{1,0:T(8,128)(2,1)S(1)}, u32[]{:S(2)}, u32[]{:S(2)}) collective-permute-start(bf16[96,3584]{1,0:T(8,128)(2,1)S(1)} %get-tuple-element.946), channel_id=1, source_target_pairs={{0,32},{32,64},{64,96},{96,128},{128,160},{160,192},{192,224},{1,3... | collective-permute-start | bytes 2064392 | tf_op jit(solution)/shard_map/while/body/eval_jaxpr/ppermute | solution.py:38
  232.5 11.3 %collective-permute-done = bf16[96,3584]{1,0:T(8,128)(2,1)S(1)} collective-permute-done((bf16[96,3584]{1,0:T(8,128)(2,1)S(1)}, bf16[96,3584]{1,0:T(8,128)(2,1)S(1)}, u32[]{:S(2)}, u32[]{:S(2)}) %collective-permute-start) | collective-permute-done | bytes 688160 | tf_op jit(solution)/shard_map/while/body/eval_jaxpr/ppermute | solution.py:38
  245.3 4.1 collective-permute-start
  251.2 10.4 %collective-permute-done = bf16[96,3584]{1,0:T(8,128)(2,1)S(1)} collective-permute-done((bf16[96,3584]{1,0:T(8,128)(2,1)S(1)}, bf16[96,3584]{1,0:T(8,128)(2,1)S(1)}, u32[]{:S(2)}, u32[]{:S(2)}) %collective-permute-start) | collective-permute-done | bytes 688160 | tf_op jit(solution)/shard_map/while/body/eval_jaxpr/ppermute | solution.py:38
  263.1 20.2 %collective-permute-start = (bf16[96,3584]{1,0:T(8,128)(2,1)S(1)}, bf16[96,3584]{1,0:T(8,128)(2,1)S(1)}, u32[]{:S(2)}, u32[]{:S(2)}) collective-permute-start(bf16[96,3584]{1,0:T(8,128)(2,1)S(1)} %get-tuple-element.946), channel_id=1, source_target_pairs={{0,32},{32,64},{64,96},{96,128},{128,160},{160,192},{192,224},{1,3... | collective-permute-start | bytes 2064392 | tf_op jit(solution)/shard_map/while/body/eval_jaxpr/ppermute | solution.py:38
  285.1 9.9 %collective-permute-done = bf16[96,3584]{1,0:T(8,128)(2,1)S(1)} collective-permute-done((bf16[96,3584]{1,0:T(8,128)(2,1)S(1)}, bf16[96,3584]{1,0:T(8,128)(2,1)S(1)}, u32[]{:S(2)}, u32[]{:S(2)}) %collective-permute-start) | collective-permute-done | bytes 688160 | tf_op jit(solution)/shard_map/while/body/eval_jaxpr/ppermute | solution.py:38
  296.4 4.1 collective-permute-start
  302.3 9.0 collective-permute-done
  312.8 20.4 %collective-permute-start = (bf16[96,3584]{1,0:T(8,128)(2,1)S(1)}, bf16[96,3584]{1,0:T(8,128)(2,1)S(1)}, u32[]{:S(2)}, u32[]{:S(2)}) collective-permute-start(bf16[96,3584]{1,0:T(8,128)(2,1)S(1)} %get-tuple-element.946), channel_id=1, source_target_pairs={{0,32},{32,64},{64,96},{96,128},{128,160},{160,192},{192,224},{1,3... | collective-permute-start | bytes 2064392 | tf_op jit(solution)/shard_map/while/body/eval_jaxpr/ppermute | solution.py:38
  335.0 8.4 collective-permute-done
  344.9 4.1 collective-permute-start
  350.8 7.5 collective-permute-done
  359.9 23.2 %collective-permute-start = (bf16[96,3584]{1,0:T(8,128)(2,1)S(1)}, bf16[96,3584]{1,0:T(8,128)(2,1)S(1)}, u32[]{:S(2)}, u32[]{:S(2)}) collective-permute-start(bf16[96,3584]{1,0:T(8,128)(2,1)S(1)} %get-tuple-element.946), channel_id=1, source_target_pairs={{0,32},{32,64},{64,96},{96,128},{128,160},{160,192},{192,224},{1,3... | collective-permute-start | bytes 2064392 | tf_op jit(solution)/shard_map/while/body/eval_jaxpr/ppermute | solution.py:38
  384.9 7.0 collective-permute-done
  391.8 1.6 gather_fusion
  395.5 12.1 %all-to-all-start = ((bf16[32,2,2,3584]{3,2,1,0:T(2,128)(2,1)}), bf16[32,2,2,3584]{3,2,1,0:T(2,128)(2,1)S(1)}, u32[]{:S(2)}, u32[]{:S(2)}) async-start(bf16[32,2,2,3584]{3,2,1,0:T(2,128)(2,1)} %broadcast_in_dim.167), calls=%async_computation | async-start | bytes 1835008 | tf_op jit(solution)/shard_map/all_to_all | solution.py:43
  409.2 1.8 all-reduce.7
  414.2 8.9 all-reduce.8
  423.3 6.7 all-reduce.9
  435.4 516.8 %while.36 = (s32[]{:T(128)}, bf16[96,3584]{1,0:T(8,128)(2,1)S(1)}, bf16[2,96,3584]{2,1,0:T(8,128)(2,1)}, s32[]{:T(128)}, pred[]{:T(512)}, /*index=5*/bf16[2,96,3...) while((s32[]{:T(128)}, bf16[96,3584]{1,0:T(8,128)(2,1)S(1)}, ...), condition=%wide.region_18.19_spmd, body=%wide.region_11.18_spmd.sunk | while | flops 2254882304 | bytes 64684780 | solution.py:229
  439.9 14.5 %collective-permute-done.1 = bf16[96,3584]{1,0:T(8,128)(2,1)S(1)} collective-permute-done((bf16[96,3584]{1,0:T(8,128)(2,1)S(1)}, bf16[96,3584]{1,0:T(8,128)(2,1)S(1)}, u32[]{:S(2)}, u32[]{:S(2)}) %collective-permute-start.1) | collective-permute-done | bytes 688160 | tf_op jit(solution)/shard_map/while/body/eval_jaxpr/ppermute | solution.py:38
  458.7 27.6 %collective-permute-done.1 = bf16[96,3584]{1,0:T(8,128)(2,1)S(1)} collective-permute-done((bf16[96,3584]{1,0:T(8,128)(2,1)S(1)}, bf16[96,3584]{1,0:T(8,128)(2,1)S(1)}, u32[]{:S(2)}, u32[]{:S(2)}) %collective-permute-start.1) | collective-permute-done | bytes 688160 | tf_op jit(solution)/shard_map/while/body/eval_jaxpr/ppermute | solution.py:38
  490.5 13.4 %collective-permute-done.1 = bf16[96,3584]{1,0:T(8,128)(2,1)S(1)} collective-permute-done((bf16[96,3584]{1,0:T(8,128)(2,1)S(1)}, bf16[96,3584]{1,0:T(8,128)(2,1)S(1)}, u32[]{:S(2)}, u32[]{:S(2)}) %collective-permute-start.1) | collective-permute-done | bytes 688160 | tf_op jit(solution)/shard_map/while/body/eval_jaxpr/ppermute | solution.py:38
  508.1 26.1 %collective-permute-done.1 = bf16[96,3584]{1,0:T(8,128)(2,1)S(1)} collective-permute-done((bf16[96,3584]{1,0:T(8,128)(2,1)S(1)}, bf16[96,3584]{1,0:T(8,128)(2,1)S(1)}, u32[]{:S(2)}, u32[]{:S(2)}) %collective-permute-start.1) | collective-permute-done | bytes 688160 | tf_op jit(solution)/shard_map/while/body/eval_jaxpr/ppermute | solution.py:38
  538.4 10.4 %collective-permute-done.1 = bf16[96,3584]{1,0:T(8,128)(2,1)S(1)} collective-permute-done((bf16[96,3584]{1,0:T(8,128)(2,1)S(1)}, bf16[96,3584]{1,0:T(8,128)(2,1)S(1)}, u32[]{:S(2)}, u32[]{:S(2)}) %collective-permute-start.1) | collective-permute-done | bytes 688160 | tf_op jit(solution)/shard_map/while/body/eval_jaxpr/ppermute | solution.py:38
  553.0 26.5 %collective-permute-done.1 = bf16[96,3584]{1,0:T(8,128)(2,1)S(1)} collective-permute-done((bf16[96,3584]{1,0:T(8,128)(2,1)S(1)}, bf16[96,3584]{1,0:T(8,128)(2,1)S(1)}, u32[]{:S(2)}, u32[]{:S(2)}) %collective-permute-start.1) | collective-permute-done | bytes 688160 | tf_op jit(solution)/shard_map/while/body/eval_jaxpr/ppermute | solution.py:38
  583.8 268.4 %collective-permute-done.1 = bf16[96,3584]{1,0:T(8,128)(2,1)S(1)} collective-permute-done((bf16[96,3584]{1,0:T(8,128)(2,1)S(1)}, bf16[96,3584]{1,0:T(8,128)(2,1)S(1)}, u32[]{:S(2)}, u32[]{:S(2)}) %collective-permute-start.1) | collective-permute-done | bytes 688160 | tf_op jit(solution)/shard_map/while/body/eval_jaxpr/ppermute | solution.py:38
  853.3 37.0 %conditional.5 = (bf16[96,3584]{1,0:T(8,128)(2,1)S(1)}) conditional(s32[]{:T(128)} %convert_element_type.383, bf16[96,3584]{1,0:T(8,128)(2,1)S(1)} %bitcast_select_fusion.7, (bf16[96,3584]{1,0:T(8,128)(2,1)S(1)}, bf16[896,3584]{1,0:T(8,128)(2,1)}, s32[]{:T(128)}, s32[4]{0:T(128)}, bf16[2,96,3584]{2,1,0:T(8,128)(2,1)S(1)}, ...), branch_computations={%region_12.12_spmd, %region_13.17_spmd} | conditional | flops 2254194176 | bytes 45416836 | solution.py:220
  854.4 4.9 fusion.39
  865.2 1.6 bitcast_reduce_fusion
  868.2 5.5 convolution_convert_fusion.4
  875.1 1.5 fusion.46
  878.4 1.6 fusion.30
  882.0 1.5 fusion.35
  883.7 6.1 fusion.27
  893.4 8.9 collective-permute-done.1
  903.4 37.0 %conditional.5 = (bf16[96,3584]{1,0:T(8,128)(2,1)S(1)}) conditional(s32[]{:T(128)} %convert_element_type.383, bf16[96,3584]{1,0:T(8,128)(2,1)S(1)} %bitcast_select_fusion.7, (bf16[96,3584]{1,0:T(8,128)(2,1)S(1)}, bf16[896,3584]{1,0:T(8,128)(2,1)}, s32[]{:T(128)}, s32[4]{0:T(128)}, bf16[2,96,3584]{2,1,0:T(8,128)(2,1)S(1)}, ...), branch_computations={%region_12.12_spmd, %region_13.17_spmd} | conditional | flops 2254194176 | bytes 45416836 | solution.py:220
  904.5 4.9 fusion.39
  915.3 1.6 bitcast_reduce_fusion
  918.3 5.6 convolution_convert_fusion.4
  925.2 1.5 fusion.46
  928.5 1.6 fusion.30
  932.1 1.5 fusion.35
  933.8 6.1 fusion.27
  943.5 8.6 collective-permute-done.1
  (409 shorter events, 124.0 us)
Async XLA Ops:
  6.5 80.4 %all-gather.3.cloned.1.call-start = ((), (), s32[]{:S(2)}) async-start(), calls=%async_computation.1 | async-start | bytes 15138816 | tf_op jit(solution)/shard_map/all_gather | solution.py:27
  135.5 258.1 %copy-start.15 = (f32[3584]{0:T(1024)S(1)}, f32[3584]{0:T(1024)}, u32[]{:S(2)}) copy-start(f32[3584]{0:T(1024)} %param.19) | copy-start | bytes 43012
  154.7 16.1 %collective-permute-start = (bf16[96,3584]{1,0:T(8,128)(2,1)S(1)}, bf16[96,3584]{1,0:T(8,128)(2,1)S(1)}, u32[]{:S(2)}, u32[]{:S(2)}) collective-permute-start(bf16[96,3584]{1,0:T(8,128)(2,1)S(1)} %get-tuple-element.946), channel_id=1, source_target_pairs={{0,32},{32,64},{64,96},{96,128},{128,160},{160,192},{192,224},{1,3... | collective-permute-start | bytes 2064392 | tf_op jit(solution)/shard_map/while/body/eval_jaxpr/ppermute | solution.py:38
  157.7 13.0 %copy-start.5 = (bf16[2,96,3584]{2,1,0:T(8,128)(2,1)}, bf16[2,96,3584]{2,1,0:T(8,128)(2,1)S(1)}, u32[]{:S(2)}) copy-start(bf16[2,96,3584]{2,1,0:T(8,128)(2,1)S(1)} %bitcast_dynamic-update-slice_fusion.7) | copy-start | bytes 4128772 | tf_op jit(solution)/shard_map/while
  189.7 18.0 %collective-permute-start = (bf16[96,3584]{1,0:T(8,128)(2,1)S(1)}, bf16[96,3584]{1,0:T(8,128)(2,1)S(1)}, u32[]{:S(2)}, u32[]{:S(2)}) collective-permute-start(bf16[96,3584]{1,0:T(8,128)(2,1)S(1)} %get-tuple-element.946), channel_id=1, source_target_pairs={{0,32},{32,64},{64,96},{96,128},{128,160},{160,192},{192,224},{1,3... | collective-permute-start | bytes 2064392 | tf_op jit(solution)/shard_map/while/body/eval_jaxpr/ppermute | solution.py:38
  195.5 12.2 %copy-start.5 = (bf16[2,96,3584]{2,1,0:T(8,128)(2,1)}, bf16[2,96,3584]{2,1,0:T(8,128)(2,1)S(1)}, u32[]{:S(2)}) copy-start(bf16[2,96,3584]{2,1,0:T(8,128)(2,1)S(1)} %bitcast_dynamic-update-slice_fusion.7) | copy-start | bytes 4128772 | tf_op jit(solution)/shard_map/while
  209.2 34.6 %collective-permute-start = (bf16[96,3584]{1,0:T(8,128)(2,1)S(1)}, bf16[96,3584]{1,0:T(8,128)(2,1)S(1)}, u32[]{:S(2)}, u32[]{:S(2)}) collective-permute-start(bf16[96,3584]{1,0:T(8,128)(2,1)S(1)} %get-tuple-element.946), channel_id=1, source_target_pairs={{0,32},{32,64},{64,96},{96,128},{128,160},{160,192},{192,224},{1,3... | collective-permute-start | bytes 2064392 | tf_op jit(solution)/shard_map/while/body/eval_jaxpr/ppermute | solution.py:38
  232.5 11.3 %copy-start.5 = (bf16[2,96,3584]{2,1,0:T(8,128)(2,1)}, bf16[2,96,3584]{2,1,0:T(8,128)(2,1)S(1)}, u32[]{:S(2)}) copy-start(bf16[2,96,3584]{2,1,0:T(8,128)(2,1)S(1)} %bitcast_dynamic-update-slice_fusion.7) | copy-start | bytes 4128772 | tf_op jit(solution)/shard_map/while
  245.3 16.3 %collective-permute-start = (bf16[96,3584]{1,0:T(8,128)(2,1)S(1)}, bf16[96,3584]{1,0:T(8,128)(2,1)S(1)}, u32[]{:S(2)}, u32[]{:S(2)}) collective-permute-start(bf16[96,3584]{1,0:T(8,128)(2,1)S(1)} %get-tuple-element.946), channel_id=1, source_target_pairs={{0,32},{32,64},{64,96},{96,128},{128,160},{160,192},{192,224},{1,3... | collective-permute-start | bytes 2064392 | tf_op jit(solution)/shard_map/while/body/eval_jaxpr/ppermute | solution.py:38
  249.5 1.5 copy-start.4
  251.2 10.4 %copy-start.5 = (bf16[2,96,3584]{2,1,0:T(8,128)(2,1)}, bf16[2,96,3584]{2,1,0:T(8,128)(2,1)S(1)}, u32[]{:S(2)}) copy-start(bf16[2,96,3584]{2,1,0:T(8,128)(2,1)S(1)} %bitcast_dynamic-update-slice_fusion.7) | copy-start | bytes 4128772 | tf_op jit(solution)/shard_map/while
  263.1 31.8 %collective-permute-start = (bf16[96,3584]{1,0:T(8,128)(2,1)S(1)}, bf16[96,3584]{1,0:T(8,128)(2,1)S(1)}, u32[]{:S(2)}, u32[]{:S(2)}) collective-permute-start(bf16[96,3584]{1,0:T(8,128)(2,1)S(1)} %get-tuple-element.946), channel_id=1, source_target_pairs={{0,32},{32,64},{64,96},{96,128},{128,160},{160,192},{192,224},{1,3... | collective-permute-start | bytes 2064392 | tf_op jit(solution)/shard_map/while/body/eval_jaxpr/ppermute | solution.py:38
  285.1 9.9 %copy-start.5 = (bf16[2,96,3584]{2,1,0:T(8,128)(2,1)}, bf16[2,96,3584]{2,1,0:T(8,128)(2,1)S(1)}, u32[]{:S(2)}) copy-start(bf16[2,96,3584]{2,1,0:T(8,128)(2,1)S(1)} %bitcast_dynamic-update-slice_fusion.7) | copy-start | bytes 4128772 | tf_op jit(solution)/shard_map/while
  296.4 14.9 %collective-permute-start = (bf16[96,3584]{1,0:T(8,128)(2,1)S(1)}, bf16[96,3584]{1,0:T(8,128)(2,1)S(1)}, u32[]{:S(2)}, u32[]{:S(2)}) collective-permute-start(bf16[96,3584]{1,0:T(8,128)(2,1)S(1)} %get-tuple-element.946), channel_id=1, source_target_pairs={{0,32},{32,64},{64,96},{96,128},{128,160},{160,192},{192,224},{1,3... | collective-permute-start | bytes 2064392 | tf_op jit(solution)/shard_map/while/body/eval_jaxpr/ppermute | solution.py:38
  302.3 9.0 copy-start.5
  312.8 30.6 %collective-permute-start = (bf16[96,3584]{1,0:T(8,128)(2,1)S(1)}, bf16[96,3584]{1,0:T(8,128)(2,1)S(1)}, u32[]{:S(2)}, u32[]{:S(2)}) collective-permute-start(bf16[96,3584]{1,0:T(8,128)(2,1)S(1)} %get-tuple-element.946), channel_id=1, source_target_pairs={{0,32},{32,64},{64,96},{96,128},{128,160},{160,192},{192,224},{1,3... | collective-permute-start | bytes 2064392 | tf_op jit(solution)/shard_map/while/body/eval_jaxpr/ppermute | solution.py:38
  335.0 8.4 copy-start.5
  344.9 13.4 %collective-permute-start = (bf16[96,3584]{1,0:T(8,128)(2,1)S(1)}, bf16[96,3584]{1,0:T(8,128)(2,1)S(1)}, u32[]{:S(2)}, u32[]{:S(2)}) collective-permute-start(bf16[96,3584]{1,0:T(8,128)(2,1)S(1)} %get-tuple-element.946), channel_id=1, source_target_pairs={{0,32},{32,64},{64,96},{96,128},{128,160},{160,192},{192,224},{1,3... | collective-permute-start | bytes 2064392 | tf_op jit(solution)/shard_map/while/body/eval_jaxpr/ppermute | solution.py:38
  350.8 7.6 copy-start.5
  359.9 31.9 %collective-permute-start = (bf16[96,3584]{1,0:T(8,128)(2,1)S(1)}, bf16[96,3584]{1,0:T(8,128)(2,1)S(1)}, u32[]{:S(2)}, u32[]{:S(2)}) collective-permute-start(bf16[96,3584]{1,0:T(8,128)(2,1)S(1)} %get-tuple-element.946), channel_id=1, source_target_pairs={{0,32},{32,64},{64,96},{96,128},{128,160},{160,192},{192,224},{1,3... | collective-permute-start | bytes 2064392 | tf_op jit(solution)/shard_map/while/body/eval_jaxpr/ppermute | solution.py:38
  384.8 7.0 copy-start.5
  394.1 13.5 %copy-start.25 = (u32[256]{0:T(256)S(1)}, u32[256]{0:T(256)}, u32[]{:S(2)}) copy-start(u32[256]{0:T(256)} %constant.280) | copy-start | bytes 3076
  394.1 14.8 %copy-start.22 = (s32[2]{0:T(128)S(1)}, s32[2]{0:T(128)}, u32[]{:S(2)}) copy-start(s32[2]{0:T(128)} %param.21) | copy-start | bytes 28
  394.1 16.9 %copy-start.24 = (u32[256]{0:T(256)S(1)}, u32[256]{0:T(256)}, u32[]{:S(2)}) copy-start(u32[256]{0:T(256)} %constant.285) | copy-start | bytes 3076
  394.1 17.5 %copy-start.23 = (u32[256]{0:T(256)S(1)}, u32[256]{0:T(256)}, u32[]{:S(2)}) copy-start(u32[256]{0:T(256)} %constant.290) | copy-start | bytes 3076
  395.5 34.5 %all-to-all-start = ((bf16[32,2,2,3584]{3,2,1,0:T(2,128)(2,1)}), bf16[32,2,2,3584]{3,2,1,0:T(2,128)(2,1)S(1)}, u32[]{:S(2)}, u32[]{:S(2)}) async-start(bf16[32,2,2,3584]{3,2,1,0:T(2,128)(2,1)} %broadcast_in_dim.167), calls=%async_computation | async-start | bytes 1835008 | tf_op jit(solution)/shard_map/all_to_all | solution.py:43
  436.8 17.6 %collective-permute-start.1 = (bf16[96,3584]{1,0:T(8,128)(2,1)S(1)}, bf16[96,3584]{1,0:T(8,128)(2,1)S(1)}, u32[]{:S(2)}, u32[]{:S(2)}) collective-permute-start(bf16[96,3584]{1,0:T(8,128)(2,1)S(1)} %get-tuple-element.947), channel_id=1, source_target_pairs={{32,0},{64,32},{96,64},{128,96},{160,128},{192,160},{224,192},{33,... | collective-permute-start | bytes 2064392 | tf_op jit(solution)/shard_map/while/body/eval_jaxpr/ppermute | solution.py:38
  439.9 14.5 %copy-start.8 = (bf16[2,96,3584]{2,1,0:T(8,128)(2,1)}, bf16[2,96,3584]{2,1,0:T(8,128)(2,1)S(1)}, u32[]{:S(2)}) copy-start(bf16[2,96,3584]{2,1,0:T(8,128)(2,1)S(1)} %bitcast_dynamic-update-slice_fusion.8) | copy-start | bytes 4128772 | tf_op jit(solution)/shard_map/while
  455.6 30.6 %collective-permute-start.1 = (bf16[96,3584]{1,0:T(8,128)(2,1)S(1)}, bf16[96,3584]{1,0:T(8,128)(2,1)S(1)}, u32[]{:S(2)}, u32[]{:S(2)}) collective-permute-start(bf16[96,3584]{1,0:T(8,128)(2,1)S(1)} %get-tuple-element.947), channel_id=1, source_target_pairs={{32,0},{64,32},{96,64},{128,96},{160,128},{192,160},{224,192},{33,... | collective-permute-start | bytes 2064392 | tf_op jit(solution)/shard_map/while/body/eval_jaxpr/ppermute | solution.py:38
  458.6 27.6 %copy-start.8 = (bf16[2,96,3584]{2,1,0:T(8,128)(2,1)}, bf16[2,96,3584]{2,1,0:T(8,128)(2,1)S(1)}, u32[]{:S(2)}) copy-start(bf16[2,96,3584]{2,1,0:T(8,128)(2,1)S(1)} %bitcast_dynamic-update-slice_fusion.8) | copy-start | bytes 4128772 | tf_op jit(solution)/shard_map/while
  487.4 16.4 %collective-permute-start.1 = (bf16[96,3584]{1,0:T(8,128)(2,1)S(1)}, bf16[96,3584]{1,0:T(8,128)(2,1)S(1)}, u32[]{:S(2)}, u32[]{:S(2)}) collective-permute-start(bf16[96,3584]{1,0:T(8,128)(2,1)S(1)} %get-tuple-element.947), channel_id=1, source_target_pairs={{32,0},{64,32},{96,64},{128,96},{160,128},{192,160},{224,192},{33,... | collective-permute-start | bytes 2064392 | tf_op jit(solution)/shard_map/while/body/eval_jaxpr/ppermute | solution.py:38
  490.5 13.4 %copy-start.8 = (bf16[2,96,3584]{2,1,0:T(8,128)(2,1)}, bf16[2,96,3584]{2,1,0:T(8,128)(2,1)S(1)}, u32[]{:S(2)}) copy-start(bf16[2,96,3584]{2,1,0:T(8,128)(2,1)S(1)} %bitcast_dynamic-update-slice_fusion.8) | copy-start | bytes 4128772 | tf_op jit(solution)/shard_map/while
  505.0 29.2 %collective-permute-start.1 = (bf16[96,3584]{1,0:T(8,128)(2,1)S(1)}, bf16[96,3584]{1,0:T(8,128)(2,1)S(1)}, u32[]{:S(2)}, u32[]{:S(2)}) collective-permute-start(bf16[96,3584]{1,0:T(8,128)(2,1)S(1)} %get-tuple-element.947), channel_id=1, source_target_pairs={{32,0},{64,32},{96,64},{128,96},{160,128},{192,160},{224,192},{33,... | collective-permute-start | bytes 2064392 | tf_op jit(solution)/shard_map/while/body/eval_jaxpr/ppermute | solution.py:38
  508.1 26.1 %copy-start.8 = (bf16[2,96,3584]{2,1,0:T(8,128)(2,1)}, bf16[2,96,3584]{2,1,0:T(8,128)(2,1)S(1)}, u32[]{:S(2)}) copy-start(bf16[2,96,3584]{2,1,0:T(8,128)(2,1)S(1)} %bitcast_dynamic-update-slice_fusion.8) | copy-start | bytes 4128772 | tf_op jit(solution)/shard_map/while
  535.4 13.4 %collective-permute-start.1 = (bf16[96,3584]{1,0:T(8,128)(2,1)S(1)}, bf16[96,3584]{1,0:T(8,128)(2,1)S(1)}, u32[]{:S(2)}, u32[]{:S(2)}) collective-permute-start(bf16[96,3584]{1,0:T(8,128)(2,1)S(1)} %get-tuple-element.947), channel_id=1, source_target_pairs={{32,0},{64,32},{96,64},{128,96},{160,128},{192,160},{224,192},{33,... | collective-permute-start | bytes 2064392 | tf_op jit(solution)/shard_map/while/body/eval_jaxpr/ppermute | solution.py:38
  538.4 10.4 %copy-start.8 = (bf16[2,96,3584]{2,1,0:T(8,128)(2,1)}, bf16[2,96,3584]{2,1,0:T(8,128)(2,1)S(1)}, u32[]{:S(2)}) copy-start(bf16[2,96,3584]{2,1,0:T(8,128)(2,1)S(1)} %bitcast_dynamic-update-slice_fusion.8) | copy-start | bytes 4128772 | tf_op jit(solution)/shard_map/while
  550.0 29.5 %collective-permute-start.1 = (bf16[96,3584]{1,0:T(8,128)(2,1)S(1)}, bf16[96,3584]{1,0:T(8,128)(2,1)S(1)}, u32[]{:S(2)}, u32[]{:S(2)}) collective-permute-start(bf16[96,3584]{1,0:T(8,128)(2,1)S(1)} %get-tuple-element.947), channel_id=1, source_target_pairs={{32,0},{64,32},{96,64},{128,96},{160,128},{192,160},{224,192},{33,... | collective-permute-start | bytes 2064392 | tf_op jit(solution)/shard_map/while/body/eval_jaxpr/ppermute | solution.py:38
  553.0 26.5 %copy-start.8 = (bf16[2,96,3584]{2,1,0:T(8,128)(2,1)}, bf16[2,96,3584]{2,1,0:T(8,128)(2,1)S(1)}, u32[]{:S(2)}) copy-start(bf16[2,96,3584]{2,1,0:T(8,128)(2,1)S(1)} %bitcast_dynamic-update-slice_fusion.8) | copy-start | bytes 4128772 | tf_op jit(solution)/shard_map/while
  580.7 271.4 %collective-permute-start.1 = (bf16[96,3584]{1,0:T(8,128)(2,1)S(1)}, bf16[96,3584]{1,0:T(8,128)(2,1)S(1)}, u32[]{:S(2)}, u32[]{:S(2)}) collective-permute-start(bf16[96,3584]{1,0:T(8,128)(2,1)S(1)} %get-tuple-element.947), channel_id=1, source_target_pairs={{32,0},{64,32},{96,64},{128,96},{160,128},{192,160},{224,192},{33,... | collective-permute-start | bytes 2064392 | tf_op jit(solution)/shard_map/while/body/eval_jaxpr/ppermute | solution.py:38
  583.7 268.4 %copy-start.8 = (bf16[2,96,3584]{2,1,0:T(8,128)(2,1)}, bf16[2,96,3584]{2,1,0:T(8,128)(2,1)S(1)}, u32[]{:S(2)}) copy-start(bf16[2,96,3584]{2,1,0:T(8,128)(2,1)S(1)} %bitcast_dynamic-update-slice_fusion.8) | copy-start | bytes 4128772 | tf_op jit(solution)/shard_map/while
  853.6 5.7 copy-start.20
  862.4 2.8 copy-start.10
  862.4 2.8 copy-start.11
  865.2 2.3 copy-start.18
  873.8 2.8 copy-start.2
  875.0 4.9 copy-start
  882.0 1.6 copy-start.1
  882.0 1.6 copy-start.9
  883.6 6.1 copy-start.21
  883.6 6.1 copy-start.17
  890.4 11.9 %collective-permute-start.1 = (bf16[96,3584]{1,0:T(8,128)(2,1)S(1)}, bf16[96,3584]{1,0:T(8,128)(2,1)S(1)}, u32[]{:S(2)}, u32[]{:S(2)}) collective-permute-start(bf16[96,3584]{1,0:T(8,128)(2,1)S(1)} %get-tuple-element.947), channel_id=1, source_target_pairs={{32,0},{64,32},{96,64},{128,96},{160,128},{192,160},{224,192},{33,... | collective-permute-start | bytes 2064392 | tf_op jit(solution)/shard_map/while/body/eval_jaxpr/ppermute | solution.py:38
  893.4 8.9 copy-start.8
  903.7 5.7 copy-start.20
  912.5 2.8 copy-start.10
  912.5 2.8 copy-start.11
  915.3 2.3 copy-start.18
  923.9 2.8 copy-start.2
  925.2 4.9 copy-start
  932.1 1.6 copy-start.1
  932.1 1.6 copy-start.9
  933.8 6.1 copy-start.21
  933.8 6.1 copy-start.17
  940.5 11.7 %collective-permute-start.1 = (bf16[96,3584]{1,0:T(8,128)(2,1)S(1)}, bf16[96,3584]{1,0:T(8,128)(2,1)S(1)}, u32[]{:S(2)}, u32[]{:S(2)}) collective-permute-start(bf16[96,3584]{1,0:T(8,128)(2,1)S(1)} %get-tuple-element.947), channel_id=1, source_target_pairs={{32,0},{64,32},{96,64},{128,96},{160,128},{192,160},{224,192},{33,... | collective-permute-start | bytes 2064392 | tf_op jit(solution)/shard_map/while/body/eval_jaxpr/ppermute | solution.py:38
  943.5 8.7 copy-start.8
  (31 other events, 41.8 us)
Sparse Core Ops, SparseCore 0:
  9.9 76.9 all-gather.2
where the time goes:
time: 974 us; the launch traced here: 959 us
  waiting for transfers between devices  569 us (58%)
  starting transfers between devices  127 us (13%)
  local copies, waits for them, and re-layouts  113 us (12%)
  matrix products  71.1 us (7%)
  other arithmetic  43.3 us (4%)
  blocking collectives  17.5 us (2%)
  between operations  15.6 us (2%)
    ppermute x18, waiting for transfers between devices, shifted(): lax.ppermute(value, axis, [(source, source + steps) for source in range(f...  493 us
    ppermute x18, starting transfers between devices, shifted(): lax.ppermute(value, axis, [(source, source + steps) for source in range(f...  115 us
    all_gather x1, waiting for transfers between devices, one_gather(): lines, at, gathered = (lax.all_gather(vector, axis), 0, [])  75.7 us
    dot_general x6, matrix products, attention_layer(): projected = jnp.dot(normed, weight_qkv, preferred_element_type=jnp.float32)  31.7 us
  transfers between devices with their start and end apart: 20, of which 19 were waited for; matrix products, arithmetic and copies ran while one was open for 3% of the time, Pallas kernels for 0%

commit v1 on v0

v1 whole, which is shorter than its diff:
```python
import functools

import jax
import jax.numpy as jnp
from jax import lax
from jax.experimental import pallas as pl
from jax.experimental.pallas import tpu as pltpu
from jax.sharding import Mesh
from jax.sharding import PartitionSpec as P

HEAD_DIM = 64
GROUP_HEADS = 7
KV_GROUPS = 2
DP = ("dp_0", "dp_1", "dp_2")

rope_base = 1000000.0
norm_eps = 1e-06
sharpness_divisor = 0.05
objective_coefficient = 256.0

LENGTH = 48
PAIRS = 7
F32 = jnp.float32
BF16 = jnp.bfloat16


def nn(a, b):
    return lax.dot_general(a, b, (((1,), (0,)), ((), ())), preferred_element_type=F32)


def nt(a, b):
    return lax.dot_general(a, b, (((1,), (1,)), ((), ())), preferred_element_type=F32)


def tn(a, b):
    return lax.dot_general(a, b, (((0,), (0,)), ((), ())), preferred_element_type=F32)


def lanes_of(shape):
    return lax.broadcasted_iota(jnp.int32, shape, 1)


def turned(block, cosine, sine, roll):
    lane = lanes_of(block.shape)
    swapped = jnp.where(lane % 64 < 32, roll(block, 96), roll(block, 32))
    return block * cosine + swapped * sine


def paired(rows, roll):
    lane = lanes_of(rows.shape)
    other = roll(rows, 64)
    zero = jnp.zeros_like(rows)
    low = lane < 64
    first = jnp.where(low, rows, zero)
    second = jnp.where(low, zero, rows)
    return tuple(
        jnp.concatenate(two, axis=0).astype(BF16)
        for two in (
            (first, jnp.where(low, zero, other)),
            (first, second),
            (jnp.where(low, other, zero), second),
        )
    )


SPANS = ((0, 3), (3, 4), (4, 7))


def stacked(blocks, span):
    chosen = blocks[span[0] : span[1]]
    return chosen[0] if len(chosen) == 1 else jnp.concatenate(chosen, axis=0)


def layer_forward(hidden, gain, wq, wo, cosine, sine, key_mask, roll):
    wide = hidden.astype(F32)
    inverse = lax.rsqrt(jnp.mean(wide * wide, axis=-1, keepdims=True) + norm_eps)
    normed = (wide * inverse * gain).astype(BF16)
    projected = nn(normed, wq[...])
    blocks = [projected[:, 128 * b : 128 * (b + 1)] for b in range(9)]
    turned_blocks = [turned(b, cosine, sine, roll) for b in blocks[:8]]
    queries = [b.astype(BF16) for b in turned_blocks[:PAIRS]]
    keys = turned_blocks[PAIRS].astype(BF16)
    values = blocks[8].astype(BF16)
    key_forms = paired(keys.astype(F32), roll)
    value_forms = paired(values.astype(F32), roll)
    probabilities = []
    context = []
    for span, key_form, value_form in zip(SPANS, key_forms, value_forms):
        scores = nt(stacked(queries, span), key_form) * HEAD_DIM ** (-0.5)
        weights = jnp.where(key_mask > 0, jnp.exp(scores), 0.0)
        low = lanes_of(weights.shape) < LENGTH
        sum_low = jnp.sum(jnp.where(low, weights, 0.0), axis=-1, keepdims=True)
        sum_high = jnp.sum(jnp.where(low, 0.0, weights), axis=-1, keepdims=True)
        probability = (weights / jnp.where(low, sum_low, sum_high)).astype(BF16)
        probabilities.append(probability)
        result = nn(probability, value_form).astype(BF16)
        for i in range(span[1] - span[0]):
            context.append(result[LENGTH * i : LENGTH * (i + 1)])
    branch = nn(jnp.concatenate(context, axis=1), wo[...])
    following = (wide + branch).astype(BF16)
    saved = jnp.concatenate(queries + [keys, values], axis=1)
    return following, saved, jnp.concatenate(probabilities, axis=0)


def layer_backward(grad, hidden, saved, probabilities, gain, wq, wo, cosine, sine, roll):
    queries = [saved[:, 128 * b : 128 * (b + 1)] for b in range(PAIRS)]
    key_forms = paired(saved[:, 896:1024].astype(F32), roll)
    value_forms = paired(saved[:, 1024:1152].astype(F32), roll)
    context_grad_t = nt(wo[...], grad)
    context_grads = [
        context_grad_t[128 * b : 128 * (b + 1)].T.astype(BF16) for b in range(PAIRS)
    ]
    query_grads = []
    key_parts = []
    value_parts = []
    for span, key_form, value_form in zip(SPANS, key_forms, value_forms):
        chosen = stacked(context_grads, span)
        probability = probabilities[LENGTH * span[0] : LENGTH * span[1]]
        wide_p = probability.astype(F32)
        prob_grad = nt(chosen, value_form)
        product = prob_grad * wide_p
        low = lanes_of(product.shape) < LENGTH
        sum_low = jnp.sum(jnp.where(low, product, 0.0), axis=-1, keepdims=True)
        sum_high = jnp.sum(jnp.where(low, 0.0, product), axis=-1, keepdims=True)
        score_grad = (
            wide_p * (prob_grad - jnp.where(low, sum_low, sum_high)) * HEAD_DIM ** (-0.5)
        ).astype(BF16)
        query_grad = nn(score_grad, key_form)
        for i in range(span[1] - span[0]):
            query_grads.append(query_grad[LENGTH * i : LENGTH * (i + 1)])
        key_parts.append(tn(score_grad, stacked(queries, span)))
        value_parts.append(tn(probability, chosen))

    def folded(parts):
        both, mixed, last = parts
        low_part = both[:LENGTH] + roll(both[LENGTH:], 64) + mixed[:LENGTH]
        high_part = mixed[LENGTH:] + last[LENGTH:] + roll(last[:LENGTH], 64)
        return jnp.where(lanes_of(low_part.shape) < 64, low_part, high_part)

    turned_back = [
        turned(block.astype(BF16).astype(F32), cosine, -sine, roll).astype(BF16)
        for block in query_grads + [folded(key_parts)]
    ]
    projected_grad = jnp.concatenate(turned_back + [folded(value_parts).astype(BF16)], axis=1)
    normed_grad = nt(wq[...], projected_grad).T
    wide = hidden.astype(F32)
    inverse = lax.rsqrt(jnp.mean(wide * wide, axis=-1, keepdims=True) + norm_eps)
    gained = normed_grad * gain
    inner = jnp.mean(gained * wide, axis=-1, keepdims=True)
    return (
        grad.astype(F32) + gained * inverse - wide * (inverse * inverse * inverse * inner)
    ).astype(BF16)


def tpu_roll(x, shift):
    return pltpu.roll(x, shift, axis=1)


def meet(axis):
    me = lax.axis_index(axis)
    count = lax.axis_size(axis)
    barrier = pltpu.get_barrier_semaphore()
    for step in (1, count - 1):
        pl.semaphore_signal(
            barrier,
            inc=1,
            device_id={axis: lax.rem(me + step, count)},
            device_id_type=pl.DeviceIdType.MESH,
        )
    pl.semaphore_wait(barrier, 2)


def forward_kernel(
    entry, gain, wq, wo, cosine, sine, key_mask, last_mask,
    hidden_out, saved_out, prob_out, last_out,
    inbox, outbox, send_sem, recv_sem,
):
    me = lax.axis_index("section")
    count = lax.axis_size("section")
    micros = entry.shape[0]
    meet("section")

    def hop(m):
        return pltpu.make_async_remote_copy(
            src_ref=outbox.at[m],
            dst_ref=inbox.at[m],
            send_sem=send_sem.at[m],
            recv_sem=recv_sem.at[m],
            device_id={"section": lax.rem(me + 1, count)},
            device_id_type=pl.DeviceIdType.MESH,
        )

    def step(m, carry):
        @pl.when(me == 0)
        def _():
            hidden_out[m] = entry[m]

        @pl.when(me > 0)
        def _():
            hop(m).wait_recv()
            hidden_out[m] = inbox[m]

        following, saved, probabilities = layer_forward(
            hidden_out[m], gain[...], wq, wo, cosine[...], sine[...], key_mask[m], tpu_roll
        )
        outbox[m] = following

        @pl.when(me < count - 1)
        def _():
            hop(m).start()

        saved_out[m] = saved
        prob_out[m] = probabilities
        last_out[m] = jnp.sum(following.astype(F32) * last_mask[m], axis=0, keepdims=True)
        return carry

    lax.fori_loop(0, micros, step, 0)

    @pl.when(me < count - 1)
    def _():
        for m in range(micros):
            hop(m).wait_send()


def backward_kernel(
    last_grad, hidden_in, saved_in, prob_in, gain, wq, wo, cosine, sine, last_mask,
    grad_out,
    inbox, outbox, send_sem, recv_sem,
):
    me = lax.axis_index("section")
    count = lax.axis_size("section")
    micros = hidden_in.shape[0]
    meet("section")

    def hop(m):
        return pltpu.make_async_remote_copy(
            src_ref=outbox.at[m],
            dst_ref=inbox.at[m],
            send_sem=send_sem.at[m],
            recv_sem=recv_sem.at[m],
            device_id={"section": lax.rem(me + count - 1, count)},
            device_id_type=pl.DeviceIdType.MESH,
        )

    def step(m, carry):
        @pl.when(me == count - 1)
        def _():
            outbox[m] = jnp.where(last_mask[m] > 0, last_grad[m], 0.0).astype(BF16)

        @pl.when(me < count - 1)
        def _():
            hop(m).wait_recv()
            outbox[m] = inbox[m]

        downstream = layer_backward(
            outbox[m], hidden_in[m], saved_in[m], prob_in[m],
            gain[...], wq, wo, cosine[...], sine[...], tpu_roll,
        )
        outbox[m] = downstream

        @pl.when(me > 0)
        def _():
            hop(m).start()

        grad_out[m] = downstream
        return carry

    lax.fori_loop(0, micros, step, 0)

    @pl.when(me > 0)
    def _():
        for m in range(micros):
            hop(m).wait_send()


def whole():
    return pl.BlockSpec(memory_space=pltpu.VMEM)


def run_kernel(body, out_shapes, scratch, ident, args):
    return pl.pallas_call(
        body,
        out_shape=out_shapes,
        in_specs=[whole()] * len(args),
        out_specs=jax.tree.map(lambda _: whole(), out_shapes),
        scratch_shapes=scratch,
        compiler_params=pltpu.CompilerParams(
            collective_id=ident, has_side_effects=True, vmem_limit_bytes=64000 * 1024
        ),
    )(*args)


def rms_scale(values, gain_row):
    return (
        values * lax.rsqrt(jnp.mean(values * values, axis=-1, keepdims=True) + norm_eps) * gain_row
    )


def embed_rows(rows_in, final_gain):
    pooled = rms_scale(rows_in.astype(F32), final_gain)
    return pooled * lax.rsqrt(jnp.sum(pooled * pooled, axis=-1, keepdims=True))


def pair_terms(question, passage, positive):
    scores = jnp.dot(question, passage.T, preferred_element_type=F32) * (1.0 / sharpness_divisor)
    weights = jnp.exp(scores)
    odds = weights / jnp.sum(weights, axis=-1, keepdims=True)
    target = (
        positive[:, None] == jnp.arange(passage.shape[0], dtype=jnp.int32)[None, :]
    ).astype(F32)
    return (odds - target) * (objective_coefficient / sharpness_divisor)


def turning(length):
    half = HEAD_DIM // 2
    frequency = rope_base ** (-jnp.arange(half, dtype=F32) * (2.0 / HEAD_DIM))
    angles = jnp.arange(length, dtype=jnp.int32).astype(F32)[:, None] * frequency[None, :]
    cosine, sine = jnp.cos(angles), jnp.sin(angles)
    return (
        jnp.concatenate([cosine] * 4, axis=1),
        jnp.concatenate([-sine, sine] * 2, axis=1),
    )


def per_device(entry, norm_gain, w_qkv, w_out, final_gain, lengths, positive):
    width = entry.shape[1]
    seqs = lengths.shape[0]
    length = entry.shape[0] // seqs
    pairs = positive.shape[0]
    pair_all = lax.all_gather(positive, DP, axis=0, tiled=True)
    full_out = lax.all_gather(w_out[0], DP, axis=0, tiled=True)
    full_qkv = lax.all_gather(w_qkv[0], DP, axis=0, tiled=True)
    cosine, sine = turning(length)
    spots = jnp.arange(length, dtype=jnp.int32)
    live = (spots[None, :] < lengths[:, None]).astype(F32)
    key_mask = jnp.concatenate([live, live], axis=1)[:, None, :]
    last_mask = (spots[None, :] == lengths[:, None] - 1).astype(F32)[:, :, None]
    block = jax.ShapeDtypeStruct((seqs, length, width), BF16)
    buffers = [
        pltpu.VMEM(block.shape, BF16),
        pltpu.VMEM(block.shape, BF16),
        pltpu.SemaphoreType.DMA((seqs,)),
        pltpu.SemaphoreType.DMA((seqs,)),
    ]
    hidden, saved, probabilities, last_rows = run_kernel(
        forward_kernel,
        [
            block,
            jax.ShapeDtypeStruct((seqs, length, 1152), BF16),
            jax.ShapeDtypeStruct((seqs, PAIRS * length, 2 * length), BF16),
            jax.ShapeDtypeStruct((seqs, 1, width), F32),
        ],
        buffers,
        0,
        (entry.reshape(block.shape), norm_gain, full_qkv, full_out, cosine, sine,
         key_mask, last_mask),
    )
    last_rows = last_rows[:, 0]
    embedding, back_embed = jax.vjp(lambda rows: embed_rows(rows, final_gain), last_rows)
    low = lax.all_gather(embedding.astype(BF16), DP, axis=0, tiled=True)
    low = low.reshape(-1, 2, width)
    question, passage = low[:, 0], low[:, 1]
    replica = lax.axis_index(DP)
    coefficient = pair_terms(question, passage, pair_all)
    mine_q = lax.dynamic_slice_in_dim(coefficient, replica * pairs, pairs, 0)
    mine_d = lax.dynamic_slice_in_dim(coefficient.T, replica * pairs, pairs, 0)
    grad_q = jnp.dot(mine_q, passage.astype(F32), precision=lax.Precision.HIGHEST)
    grad_d = jnp.dot(mine_d, question.astype(F32), precision=lax.Precision.HIGHEST)
    grad_emb = jnp.stack([grad_q, grad_d], axis=1).reshape(seqs, width)
    last_grad = back_embed(grad_emb)[0]
    grads = run_kernel(
        backward_kernel,
        block,
        buffers,
        1,
        (last_grad[:, None, :], hidden, saved, probabilities, norm_gain, full_qkv, full_out,
         cosine, sine, last_mask),
    )
    return grads.reshape(1, seqs * length, width)


def solution(mesh):
    finer = Mesh(
        mesh.devices.reshape(mesh.shape["section"], 4, 4, 2), ("section", "dp_0", "dp_1", "dp_2")
    )
    in_specs = (
        P(DP, None),
        P("section", None),
        P("section", DP, None),
        P("section", DP, None),
        P(),
        P(DP),
        P(DP),
    )
    return jax.shard_map(
        per_device, mesh=finer, in_specs=in_specs, out_specs=P("section", DP, None),
        check_vma=False,
    )
```

time: 974 us -> 450 us (0.46); the launches traced: 959 us -> 447 us
  waiting for transfers between devices: 569 us -> 104 us
  Pallas kernels: 0 us -> 263 us
  starting transfers between devices: 127 us -> 0.04 us
  local copies, waits for them, and re-layouts: 113 us -> 17.4 us
  matrix products: 71.1 us -> 1.02 us
  other arithmetic: 43.3 us -> 7.35 us
  blocking collectives: 17.5 us -> 40.1 us
    ppermute x18 -> x0, waiting for transfers between devices: 493 us -> none  [shifted(): lax.ppermute(value, axis, [(source, source + steps) for source in range(f...]
    pallas_call x0 -> x2, Pallas kernels: none -> 263 us  [run_kernel(): pl.pallas_call(body, out_shape=out_shapes, in_specs=[whole()] * len(args)...]
    ppermute x18 -> x0, starting transfers between devices: 115 us -> none  [shifted(): lax.ppermute(value, axis, [(source, source + steps) for source in range(f...]
    dot_general x27 -> x3, matrix products: 71.1 us -> 1.02 us  [the longest x1 0.42 us: per_device(): jnp.dot(mine_q, passage.astype(F32), precision=lax.Precision.HIGHEST)]
    all_gather x1 -> x2, waiting for transfers between devices: 75.7 us -> 104 us  [the longest x1 53 us: per_device(): full_out = lax.all_gather(w_out[0], DP, axis=0, tiled=True)]
    dynamic_slice x32 -> x0, local copies, waits for them, and re-layouts: 26 us -> none  [the longest x9 11.3 us: backward_tick(): grad_buf[slot_id]]
    all_gather x0 -> x1, blocking collectives: none -> 25.7 us  [per_device(): low = lax.all_gather(embedding.astype(BF16), DP, axis=0, tiled=True)]
    another operation x14 -> x1, local copies, waits for them, and re-layouts: 24.8 us -> 0.03 us  [per_device(): grad_emb = jnp.stack([grad_q, grad_d], axis=1).reshape(seqs, width)]
  transfers between devices with their start and end apart: 20 -> 2, of which waited for: 19 -> 2; matrix products, arithmetic and copies ran while one was open for 3% -> 3% of each run, Pallas kernels for 0% -> 0%
where the time goes in v1:
time: 450 us; the launch traced here: 447 us
  Pallas kernels  263 us (58%)
  waiting for transfers between devices  104 us (23%)
  blocking collectives  40.1 us (9%)
  local copies, waits for them, and re-layouts  17.4 us (4%)
  between operations  14.1 us (3%)
  other arithmetic  7.35 us (2%)
    pallas_call x2, Pallas kernels, run_kernel(): pl.pallas_call(body, out_shape=out_shapes, in_specs=[whole()] * len(args)...  263 us
    all_gather x1, waiting for transfers between devices, per_device(): full_out = lax.all_gather(w_out[0], DP, axis=0, tiled=True)  53 us
    all_gather x1, waiting for transfers between devices, per_device(): full_qkv = lax.all_gather(w_qkv[0], DP, axis=0, tiled=True)  50.7 us
    all_gather x1, blocking collectives, per_device(): low = lax.all_gather(embedding.astype(BF16), DP, axis=0, tiled=True)  25.7 us
    unnamed x12, local copies, waits for them, and re-layouts  15.6 us
    unnamed x1, blocking collectives  14.4 us
  transfers between devices with their start and end apart: 2, of which 2 were waited for; matrix products, arithmetic and copies ran while one was open for 3% of the time, Pallas kernels for 0%

profile of v1, /device:TPU:1, one launch (start us, length us, event | category | flops | bytes accessed | tf_op | source)
XLA Modules:
  0.0 447.4 jit_solution(16770616820880241363)
XLA Ops:
  6.5 0.0 copy-start.2
  6.5 0.0 all-gather.8.cloned.1.call-start
  6.5 2.0 copy.17
  8.5 0.0 all-gather.8.cloned.1.call-update
  8.6 0.0 all-gather.6.cloned.1.call-start
  8.6 0.7 all-gather.6.cloned.1.call-update
  9.3 1.3 dynamic-slice.4
  11.2 0.9 dynamic-update-slice
  12.1 14.4 %all-reduce = s32[64]{0:T(128)S(1)} all-reduce(s32[64]{0:T(128)S(1)} %dynamic-update-slice), channel_id=1, replica_groups=mesh['section'=8,'dp_0'=4,'dp_1'=4,'dp_2'=2] {'dp_0','dp_1','dp_2'}, use_global_device_ids=true, to_apply=%add | all-reduce | flops 64 | bytes 512
  26.5 0.7 iota_compare_fusion.2
  27.3 0.7 add_convert_fusion
  27.9 0.2 fusion.18
  28.1 0.7 pad_maximum_fusion.1
  28.8 0.0 copy-done.2
  28.8 0.7 fusion.9.last_mask
  29.6 53.0 %all-gather.8.cloned.1.call-done = bf16[1,896,3584]{2,0,1:T(2,128)(2,1)} async-done(((bf16[1,28,3584]{2,0,1:T(2,128)(2,1)}), bf16[1,896,3584]{2,0,1:T(2,128)(2,1)}) %all-gather.8.cloned.1.call-update) | async-done | bytes 6422544 | tf_op jit(solution)/shard_map/all_gather | solution.py:331
  82.6 9.0 %copy.56 = bf16[1,896,3584]{2,1,0:T(8,128)(2,1)} copy(bf16[1,896,3584]{2,0,1:T(2,128)(2,1)} %all-gather.8.cloned.1.call-done) | data formatting | bytes 12845056
  91.5 50.7 %all-gather.6.cloned.1.call-done = bf16[1,3584,1152]{2,1,0:T(8,128)(2,1)} async-done(((bf16[1,112,1152]{2,1,0:T(8,128)(2,1)}), bf16[1,3584,1152]{2,1,0:T(8,128)(2,1)}) %all-gather.6.cloned.1.call-update) | async-done | bytes 8257552 | tf_op jit(solution)/shard_map/all_gather | solution.py:332
  142.3 0.0 copy-start.1
  142.3 42.8 %shard_map.73 = (bf16[4,48,3584]{2,1,0:T(8,128)(2,1)}, bf16[4,48,1152]{2,1,0:T(8,128)(2,1)}, bf16[4,336,96]{2,1,0:T(8,128)(2,1)}, f32[4,1,3584]{2,1,0:T(1,128)}) custom-call(bf16[4,48,3584]{2,1,0:T(8,128)(2,1)} %bitcast.49, f32[1,3584]{1,0:T(1,128)} %gain.3, bf16[3584,1152]{1,0:T(8,128)(2,1)} %bitcast.46, bf16[896,3584]{1,0:T(8,128)(2,1)} %bitcast.44, ...), custom_call_target="tpu_custom_call" | custom-call | tf_op jit(solution)/shard_map/pallas_call | solution.py:281
  185.1 1.0 fusion.14
  186.1 0.0 copy-done.1
  186.1 1.0 multiply_reduce_fusion.1
  187.1 0.9 fusion.17
  188.0 25.7 %all-gather.2 = bf16[32,4,3584]{2,1,0:T(4,128)(2,1)S(1)} all-gather(bf16[1,4,3584]{2,1,0:T(4,128)(2,1)S(1)} %fusion.17), channel_id=1, replica_groups=mesh['section'=8,'dp_0'=4,'dp_1'=4,'dp_2'=2] {'dp_0','dp_1','dp_2'}, dimensions={0}, use_global_device_ids=true | all-gather | bytes 946176 | tf_op jit(solution)/shard_map/all_gather | solution.py:360
  213.7 0.3 reshape.163
  214.1 1.3 fusion.23
  215.3 0.0 copy-start
  215.4 0.3 fusion.24
  215.7 0.4 convolution_bitcast_fusion.1
  216.1 0.3 convolution_bitcast_fusion
  216.5 0.1 reshape.164
  216.6 0.1 reshape.165
  216.6 0.0 copy-done
  216.6 0.2 multiply_reduce_fusion
  216.9 0.2 fusion.13
  217.1 0.9 add_add_fusion.last_grad
  218.0 220.0 %shard_map.74 = bf16[4,48,3584]{2,1,0:T(8,128)(2,1)} custom-call(f32[4,1,3584]{2,1,0:T(1,128)} %add_add_fusion.last_grad, bf16[4,48,3584]{2,1,0:T(8,128)(2,1)} %get-tuple-element.10.hidden_in, bf16[4,48,1152]{2,1,0:T(8,128)(2,1)} %get-tuple-element.11.saved_in, bf16[4,336,96]{2,1,0:T(8,128)(2,1)} %get-tuple-element.12.prob_in, f32[1,3584]{1,0:T(1,128)} %gain.3, ...), custom_call_target="tpu_custom_call" | custom-call | tf_op jit(solution)/shard_map/pallas_call | solution.py:281
  438.1 2.5 copy.59
  (11 shorter events, 0.1 us)
Async XLA Ops:
  6.5 22.3 %copy-start.2 = (s32[4]{0:T(128)S(1)}, s32[4]{0:T(128)}, u32[]{:S(2)}) copy-start(s32[4]{0:T(128)} %param.12) | copy-start | bytes 52
  6.5 76.0 %all-gather.8.cloned.1.call-start = ((), (), s32[]{:S(2)}) async-start(), calls=%async_computation.1 | async-start | bytes 13246464 | tf_op jit(solution)/shard_map/all_gather | solution.py:331
  8.6 133.7 %all-gather.6.cloned.1.call-start = ((), (), s32[]{:S(2)}) async-start(), calls=%async_computation | async-start | bytes 8515584 | tf_op jit(solution)/shard_map/all_gather | solution.py:332
  142.3 43.8 %copy-start.1 = (f32[3584]{0:T(1024)S(1)}, f32[3584]{0:T(1024)}, u32[]{:S(2)}) copy-start(f32[3584]{0:T(1024)} %param.11) | copy-start | bytes 43012
  215.3 1.3 copy-start
Sparse Core Ops, SparseCore 0:
  9.9 72.6 all-gather.7
  85.2 57.0 all-gather.5

commit v2 on v1

--- a/solution.py
+++ b/solution.py
@@ -156,52 +156,297 @@
     return pltpu.roll(x, shift, axis=1)
 
 
-def meet(axis):
-    me = lax.axis_index(axis)
-    count = lax.axis_size(axis)
+def remote(source, target, send, receive, place):
+    return pltpu.make_async_remote_copy(
+        src_ref=source,
+        dst_ref=target,
+        send_sem=send,
+        recv_sem=receive,
+        device_id=place,
+        device_id_type=pl.DeviceIdType.MESH,
+    )
+
+
+class Plane:
+    def __init__(self):
+        self.x = lax.axis_index("dp_0")
+        self.y = lax.axis_index("dp_1")
+        self.core = lax.axis_index("dp_2")
+
+    def spot(self, first, second):
+        other = 1 - self.core
+        return (
+            lax.rem(self.x + first * other + second * self.core, 4),
+            lax.rem(self.y + first * self.core + second * other, 4),
+        )
+
+    def slot(self, first, second, mine=True):
+        x, y = self.spot(first % 4, second % 4)
+        core = self.core if mine else 1 - self.core
+        return (x * 4 + y) * 2 + core
+
+    def device(self, first, second):
+        x, y = self.spot(first % 4, second % 4)
+        return {"dp_0": x, "dp_1": y}
+
+    def partner_slot(self, x, y):
+        return (x * 4 + y) * 2 + (1 - self.core)
+
+    def partner(self):
+        return {"dp_2": 1 - self.core}
+
+
+def start_meeting(plane):
+    me = lax.axis_index("section")
+    count = lax.axis_size("section")
     barrier = pltpu.get_barrier_semaphore()
-    for step in (1, count - 1):
+    places = [{"section": lax.rem(me + step, count)} for step in (1, count - 1)]
+    places.append(plane.partner())
+    places += [plane.device(a, b) for a in range(4) for b in range(4) if a or b]
+    for place in places:
         pl.semaphore_signal(
-            barrier,
-            inc=1,
-            device_id={axis: lax.rem(me + step, count)},
-            device_id_type=pl.DeviceIdType.MESH,
-        )
-    pl.semaphore_wait(barrier, 2)
-
-
-def forward_kernel(
-    entry, gain, wq, wo, cosine, sine, key_mask, last_mask,
-    hidden_out, saved_out, prob_out, last_out,
-    inbox, outbox, send_sem, recv_sem,
+            barrier, inc=1, device_id=place, device_id_type=pl.DeviceIdType.MESH
+        )
+    pl.semaphore_wait(barrier, len(places))
+
+
+class Gather:
+    def __init__(self, plane, own, whole, rows, cut, sends, receives, partner_receives):
+        self.plane, self.own, self.whole = plane, own, whole
+        self.rows, self.cut = rows, cut
+        self.sends, self.receives = sends, receives
+        self.partner_receives = partner_receives
+        self.started = []
+
+    def part(self, slot, half):
+        low, size = ((0, self.rows), (0, self.cut), (self.cut, self.rows - self.cut))[half]
+        return self.whole.at[pl.ds(pl.multiple_of(slot * self.rows + low, 16), size)]
+
+    def send(self, slot, half, place, receives=None, own=False):
+        target = self.part(slot, half)
+        receives = self.receives.at[slot // 2, max(half - 1, 0)] if receives is None else receives
+        copy = remote(
+            self.own if own else target,
+            target,
+            self.sends.at[len(self.started)],
+            receives,
+            place,
+        )
+        copy.start()
+        self.started.append(copy)
+
+    def hand_over(self, slot, own=False):
+        self.send(
+            slot, 0, self.plane.partner(), self.partner_receives.at[slot // 2], own=own
+        )
+
+    def arrived(self, slot, half):
+        part = self.part(slot, half)
+        remote(
+            part, part, self.sends.at[0], self.receives.at[slot // 2, max(half - 1, 0)],
+            self.plane.partner(),
+        ).wait_recv()
+
+    def begin(self):
+        plane = self.plane
+        slot = plane.slot(0, 0)
+        for step in (1, -1):
+            self.send(slot, 0, plane.device(step, 0), own=True)
+            self.send(slot, 0, plane.device(0, step), own=True)
+        self.hand_over(slot, own=True)
+        self.whole[pl.ds(pl.multiple_of(slot * self.rows, 16), self.rows)] = self.own[...]
+
+    def first_ring(self):
+        plane = self.plane
+        for step, half in ((-1, 1), (1, 2)):
+            slot = plane.slot(step, 0)
+            self.arrived(slot, 0)
+            self.send(slot, half, plane.device(-step, 0))
+            self.spread(slot)
+        slot = plane.slot(2, 0)
+        self.arrived(slot, 1)
+        self.arrived(slot, 2)
+        self.spread(slot)
+
+    def spread(self, slot):
+        for step in (1, -1):
+            self.send(slot, 0, self.plane.device(0, step))
+        self.hand_over(slot)
+
+    def second_ring(self):
+        plane = self.plane
+        for first in (0, -1, 1, 2):
+            for step, half in ((-1, 1), (1, 2)):
+                slot = plane.slot(first, step)
+                self.arrived(slot, 0)
+                self.send(slot, half, plane.device(0, -step))
+                self.hand_over(slot)
+        for first in (0, -1, 1, 2):
+            slot = plane.slot(first, 2)
+            self.arrived(slot, 1)
+            self.arrived(slot, 2)
+            self.hand_over(slot)
+
+    def from_partner(self):
+        for at in range(16):
+            part = self.part(self.plane.partner_slot(at // 4, at % 4), 0)
+            remote(
+                part, part, self.sends.at[0], self.partner_receives.at[at],
+                self.plane.partner(),
+            ).wait_recv()
+
+    def drain(self):
+        for copy in self.started:
+            copy.wait_send()
+
+
+GATHER_SENDS = 36
+
+
+def contrast(plane, last_rows, final_gain, positive, gathered, outgoing, sends, receives,
+             partner_receives, last_grad):
+    rows = jnp.concatenate([last_rows[m] for m in range(4)], axis=0)
+    gain = final_gain[...]
+    inverse = lax.rsqrt(jnp.mean(rows * rows, axis=-1, keepdims=True) + norm_eps)
+    pooled = rows * inverse * gain
+    scale = lax.rsqrt(jnp.sum(pooled * pooled, axis=-1, keepdims=True))
+    embedding = pooled * scale
+    tail = jnp.broadcast_to(positive[...], (4, 128))
+    packed = jnp.concatenate(
+        [
+            jnp.concatenate([embedding[:, 896 * k : 896 * (k + 1)], tail], axis=1)
+            for k in range(4)
+        ],
+        axis=0,
+    ).astype(BF16)
+    outgoing[...] = packed
+    mine = plane.slot(0, 0)
+    gathered[mine] = packed
+    started = []
+
+    def send(source, slot, receive, place):
+        copy = remote(source, gathered.at[slot], sends.at[len(started)], receive, place)
+        copy.start()
+        started.append(copy)
+
+    others = [(a, b) for a in range(4) for b in range(4) if a or b]
+    others.sort(key=lambda ab: min(ab[0], 4 - ab[0]) + min(ab[1], 4 - ab[1]))
+    for a, b in reversed(others):
+        send(outgoing, mine, receives.at[mine // 2], plane.device(a, b))
+    send(outgoing, mine, partner_receives.at[mine // 2], plane.partner())
+    for a, b in others:
+        slot = plane.slot(a, b)
+        remote(
+            outgoing, gathered.at[slot], sends.at[0], receives.at[slot // 2], plane.partner()
+        ).wait_recv()
+        send(gathered.at[slot], slot, partner_receives.at[slot // 2], plane.partner())
+    for at in range(16):
+        slot = plane.partner_slot(at // 4, at % 4)
+        remote(
+            outgoing, gathered.at[slot], sends.at[0], partner_receives.at[at], plane.partner()
+        ).wait_recv()
+    for copy in started:
+        copy.wait_send()
+
+    flat = jnp.concatenate([gathered[i] for i in range(32)], axis=0)
+    at = lax.broadcasted_iota(jnp.int32, (128, 512), 0)
+    lane = lanes_of((128, 512))
+    number = at & 63
+    row = (number >> 1) * 16 + (number & 1) * 2 + (at >> 6)
+    pieces = []
+    for k in range(4):
+        chosen = jnp.where(lane == row + 4 * k, 1.0, 0.0).astype(BF16)
+        pieces.append(nn(chosen, flat))
+    everyone = jnp.concatenate([p[:, :896] for p in pieces], axis=1).astype(BF16)
+    target = pieces[0][:64, 896:960]
+    logits = nt(everyone[:64], everyone[64:]) * (1.0 / sharpness_divisor)
+    weights = jnp.exp(logits)
+    odds = weights / jnp.sum(weights, axis=-1, keepdims=True)
+    column = lanes_of((64, 64))
+    hit = jnp.where(target == column.astype(F32), 1.0, 0.0)
+    coefficient = (odds - hit) * (objective_coefficient / sharpness_divisor)
+    turned_coefficient = coefficient.T
+    line = lax.broadcasted_iota(jnp.int32, (64, 64), 0)
+    blank = jnp.zeros((1, 64), F32)
+    replica = mine
+    chosen_rows = []
+    for m in range(4):
+        source = turned_coefficient if m % 2 else coefficient
+        one = jnp.sum(
+            jnp.where(line == replica * 2 + m // 2, source, 0.0), axis=0, keepdims=True
+        )
+        chosen_rows.append(jnp.concatenate([one, blank] if m % 2 else [blank, one], axis=1))
+    exact = jnp.concatenate(chosen_rows, axis=0)
+    top = exact.astype(BF16)
+    rest = exact - top.astype(F32)
+    middle = rest.astype(BF16)
+    low = (rest - middle.astype(F32)).astype(BF16)
+    embed_grad = nn(top, everyone) + nn(middle, everyone) + nn(low, everyone)
+    pooled_grad = embed_grad * scale - pooled * (
+        scale * scale * scale * jnp.sum(embed_grad * pooled, axis=-1, keepdims=True)
+    )
+    gained = pooled_grad * gain
+    row_grad = gained * inverse - rows * (
+        inverse * inverse * inverse * jnp.mean(gained * rows, axis=-1, keepdims=True)
+    )
+    for m in range(4):
+        last_grad[m] = row_grad[m : m + 1]
+
+
+def step_kernel(
+    entry, gain, wq_own, wo_own, cosine, sine, key_mask, last_mask, final_gain, positive,
+    spread_rows,
+    grad_out,
+    wq, wo_spaced, wo, hidden, saved, prob, last_rows, last_grad, embeds, embed_own,
+    inbox, outbox, back_inbox, back_outbox,
+    wq_send, wq_recv, wq_cross, wo_send, wo_recv, wo_cross, e_send, e_recv, e_cross,
+    f_send, f_recv, b_send, b_recv,
 ):
     me = lax.axis_index("section")
     count = lax.axis_size("section")
     micros = entry.shape[0]
-    meet("section")
+    plane = Plane()
+    start_meeting(plane)
+    gathers = (
+        Gather(plane, wq_own, wq, 112, 64, wq_send, wq_recv, wq_cross),
+        Gather(plane, wo_own, wo_spaced, 32, 16, wo_send, wo_recv, wo_cross),
+    )
+    for gather in gathers:
+        gather.begin()
+    for gather in gathers:
+        gather.first_ring()
+    for gather in gathers:
+        gather.second_ring()
+    for gather in gathers:
+        gather.from_partner()
+    for gather in gathers:
+        gather.drain()
+
+    def pack(b, carry):
+        spaced = wo_spaced[pl.ds(pl.multiple_of(b * 256, 256), 256)]
+        wo[pl.ds(pl.multiple_of(b * 224, 16), 224)] = nn(spread_rows[...], spaced).astype(BF16)
+        return carry
+
+    lax.fori_loop(0, 4, pack, 0)
 
     def hop(m):
-        return pltpu.make_async_remote_copy(
-            src_ref=outbox.at[m],
-            dst_ref=inbox.at[m],
-            send_sem=send_sem.at[m],
-            recv_sem=recv_sem.at[m],
-            device_id={"section": lax.rem(me + 1, count)},
-            device_id_type=pl.DeviceIdType.MESH,
-        )
-
-    def step(m, carry):
+        return remote(
+            outbox.at[m], inbox.at[m], f_send.at[m], f_recv.at[m],
+            {"section": lax.rem(me + 1, count)},
+        )
+
+    def forward(m, carry):
         @pl.when(me == 0)
         def _():
-            hidden_out[m] = entry[m]
+            hidden[m] = entry[m]
 
         @pl.when(me > 0)
         def _():
             hop(m).wait_recv()
-            hidden_out[m] = inbox[m]
-
-        following, saved, probabilities = layer_forward(
-            hidden_out[m], gain[...], wq, wo, cosine[...], sine[...], key_mask[m], tpu_roll
+            hidden[m] = inbox[m]
+
+        following, kept, probabilities = layer_forward(
+            hidden[m], gain[...], wq, wo, cosine[...], sine[...], key_mask[m], tpu_roll
         )
         outbox[m] = following
 
@@ -209,106 +454,62 @@
         def _():
             hop(m).start()
 
-        saved_out[m] = saved
-        prob_out[m] = probabilities
-        last_out[m] = jnp.sum(following.astype(F32) * last_mask[m], axis=0, keepdims=True)
+        saved[m] = kept
+        prob[m] = probabilities
+        last_rows[m] = jnp.sum(following.astype(F32) * last_mask[m], axis=0, keepdims=True)
         return carry
 
-    lax.fori_loop(0, micros, step, 0)
+    lax.fori_loop(0, micros, forward, 0)
 
     @pl.when(me < count - 1)
     def _():
         for m in range(micros):
             hop(m).wait_send()
 
-
-def backward_kernel(
-    last_grad, hidden_in, saved_in, prob_in, gain, wq, wo, cosine, sine, last_mask,
-    grad_out,
-    inbox, outbox, send_sem, recv_sem,
-):
-    me = lax.axis_index("section")
-    count = lax.axis_size("section")
-    micros = hidden_in.shape[0]
-    meet("section")
-
-    def hop(m):
-        return pltpu.make_async_remote_copy(
-            src_ref=outbox.at[m],
-            dst_ref=inbox.at[m],
-            send_sem=send_sem.at[m],
-            recv_sem=recv_sem.at[m],
-            device_id={"section": lax.rem(me + count - 1, count)},
-            device_id_type=pl.DeviceIdType.MESH,
-        )
-
-    def step(m, carry):
+    @pl.when(me == count - 1)
+    def _():
+        contrast(plane, last_rows, final_gain, positive, embeds, embed_own, e_send, e_recv,
+                 e_cross, last_grad)
+
+    def back_hop(m):
+        return remote(
+            back_outbox.at[m], back_inbox.at[m], b_send.at[m], b_recv.at[m],
+            {"section": lax.rem(me + count - 1, count)},
+        )
+
+    def backward(m, carry):
         @pl.when(me == count - 1)
         def _():
-            outbox[m] = jnp.where(last_mask[m] > 0, last_grad[m], 0.0).astype(BF16)
+            grad_out[m] = jnp.where(last_mask[m] > 0, last_grad[m], 0.0).astype(BF16)
 
         @pl.when(me < count - 1)
         def _():
-            hop(m).wait_recv()
-            outbox[m] = inbox[m]
+            back_hop(m).wait_recv()
+            grad_out[m] = back_inbox[m]
 
         downstream = layer_backward(
-            outbox[m], hidden_in[m], saved_in[m], prob_in[m],
+            grad_out[m], hidden[m], saved[m], prob[m],
             gain[...], wq, wo, cosine[...], sine[...], tpu_roll,
         )
-        outbox[m] = downstream
+        back_outbox[m] = downstream
 
         @pl.when(me > 0)
         def _():
-            hop(m).start()
+            back_hop(m).start()
 
         grad_out[m] = downstream
         return carry
 
-    lax.fori_loop(0, micros, step, 0)
+    lax.fori_loop(0, micros, backward, 0)
 
     @pl.when(me > 0)
     def _():
         for m in range(micros):
-            hop(m).wait_send()
+            back_hop(m).wait_send()
 
 
 def whole():
     return pl.BlockSpec(memory_space=pltpu.VMEM)
-
-
-def run_kernel(body, out_shapes, scratch, ident, args):
-    return pl.pallas_call(
-        body,
-        out_shape=out_shapes,
-        in_specs=[whole()] * len(args),
-        out_specs=jax.tree.map(lambda _: whole(), out_shapes),
-        scratch_shapes=scratch,
-        compiler_params=pltpu.CompilerParams(
-            collective_id=ident, has_side_effects=True, vmem_limit_bytes=64000 * 1024
-        ),
-    )(*args)
-
-
-def rms_scale(values, gain_row):
-    return (
-        values * lax.rsqrt(jnp.mean(values * values, axis=-1, keepdims=True) + norm_eps) * gain_row
-    )
-
-
-def embed_rows(rows_in, final_gain):
-    pooled = rms_scale(rows_in.astype(F32), final_gain)
-    return pooled * lax.rsqrt(jnp.sum(pooled * pooled, axis=-1, keepdims=True))
-
-
-def pair_terms(question, passage, positive):
-    scores = jnp.dot(question, passage.T, preferred_element_type=F32) * (1.0 / sharpness_divisor)
-    weights = jnp.exp(scores)
-    odds = weights / jnp.sum(weights, axis=-1, keepdims=True)
-    target = (
-        positive[:, None] == jnp.arange(passage.shape[0], dtype=jnp.int32)[None, :]
-    ).astype(F32)
-    return (odds - target) * (objective_coefficient / sharpness_divisor)
 
 
 def turning(length):
@@ -326,56 +527,51 @@
     width = entry.shape[1]
     seqs = lengths.shape[0]
     length = entry.shape[0] // seqs
-    pairs = positive.shape[0]
-    pair_all = lax.all_gather(positive, DP, axis=0, tiled=True)
-    full_out = lax.all_gather(w_out[0], DP, axis=0, tiled=True)
-    full_qkv = lax.all_gather(w_qkv[0], DP, axis=0, tiled=True)
     cosine, sine = turning(length)
     spots = jnp.arange(length, dtype=jnp.int32)
     live = (spots[None, :] < lengths[:, None]).astype(F32)
     key_mask = jnp.concatenate([live, live], axis=1)[:, None, :]
     last_mask = (spots[None, :] == lengths[:, None] - 1).astype(F32)[:, :, None]
-    block = jax.ShapeDtypeStruct((seqs, length, width), BF16)
-    buffers = [
-        pltpu.VMEM(block.shape, BF16),
-        pltpu.VMEM(block.shape, BF16),
-        pltpu.SemaphoreType.DMA((seqs,)),
-        pltpu.SemaphoreType.DMA((seqs,)),
-    ]
-    hidden, saved, probabilities, last_rows = run_kernel(
-        forward_kernel,
-        [
-            block,
-            jax.ShapeDtypeStruct((seqs, length, 1152), BF16),
-            jax.ShapeDtypeStruct((seqs, PAIRS * length, 2 * length), BF16),
-            jax.ShapeDtypeStruct((seqs, 1, width), F32),
+    target = jnp.repeat(positive, 2).astype(F32)[:, None]
+    packed = jnp.arange(224)
+    spread_rows = (
+        jnp.arange(256)[None, :] == (packed // 28 * 32 + packed % 28)[:, None]
+    ).astype(BF16)
+    block = (seqs, length, width)
+    dma = pltpu.SemaphoreType.DMA
+    args = (
+        entry.reshape(block), norm_gain, w_qkv[0], jnp.pad(w_out[0], ((0, 4), (0, 0))),
+        cosine, sine, key_mask, last_mask, final_gain[None, :], target, spread_rows,
+    )
+    grads = pl.pallas_call(
+        step_kernel,
+        out_shape=jax.ShapeDtypeStruct(block, BF16),
+        in_specs=[whole()] * len(args),
+        out_specs=whole(),
+        scratch_shapes=[
+            pltpu.VMEM((width, 1152), BF16),
+            pltpu.VMEM((1024, width), BF16),
+            pltpu.VMEM((896, width), BF16),
+            pltpu.VMEM(block, BF16),
+            pltpu.VMEM((seqs, length, 1152), BF16),
+            pltpu.VMEM((seqs, PAIRS * length, 2 * length), BF16),
+            pltpu.VMEM((seqs, 1, width), F32),
+            pltpu.VMEM((seqs, 1, width), F32),
+            pltpu.VMEM((32, 16, 1024), BF16),
+            pltpu.VMEM((16, 1024), BF16),
+            pltpu.VMEM(block, BF16),
+            pltpu.VMEM(block, BF16),
+            pltpu.VMEM(block, BF16),
+            pltpu.VMEM(block, BF16),
+            dma((GATHER_SENDS,)), dma((16, 2)), dma((16,)),
+            dma((GATHER_SENDS,)), dma((16, 2)), dma((16,)),
+            dma((31,)), dma((16,)), dma((16,)),
+            dma((seqs,)), dma((seqs,)), dma((seqs,)), dma((seqs,)),
         ],
-        buffers,
-        0,
-        (entry.reshape(block.shape), norm_gain, full_qkv, full_out, cosine, sine,
-         key_mask, last_mask),
-    )
-    last_rows = last_rows[:, 0]
-    embedding, back_embed = jax.vjp(lambda rows: embed_rows(rows, final_gain), last_rows)
-    low = lax.all_gather(embedding.astype(BF16), DP, axis=0, tiled=True)
-    low = low.reshape(-1, 2, width)
-    question, passage = low[:, 0], low[:, 1]
-    replica = lax.axis_index(DP)
-    coefficient = pair_terms(question, passage, pair_all)
-    mine_q = lax.dynamic_slice_in_dim(coefficient, replica * pairs, pairs, 0)
-    mine_d = lax.dynamic_slice_in_dim(coefficient.T, replica * pairs, pairs, 0)
-    grad_q = jnp.dot(mine_q, passage.astype(F32), precision=lax.Precision.HIGHEST)
-    grad_d = jnp.dot(mine_d, question.astype(F32), precision=lax.Precision.HIGHEST)
-    grad_emb = jnp.stack([grad_q, grad_d], axis=1).reshape(seqs, width)
-    last_grad = back_embed(grad_emb)[0]
-    grads = run_kernel(
-        backward_kernel,
-        block,
-        buffers,
-        1,
-        (last_grad[:, None, :], hidden, saved, probabilities, norm_gain, full_qkv, full_out,
-         cosine, sine, last_mask),
-    )
+        compiler_params=pltpu.CompilerParams(
+            collective_id=0, has_side_effects=True, vmem_limit_bytes=64000 * 1024
+        ),
+    )(*args)
     return grads.reshape(1, seqs * length, width)
 
 

time: 450 us -> 337 us (0.75)
  waiting for transfers between devices: 104 us -> 0 us
  Pallas kernels: 263 us -> 324 us
  blocking collectives: 40.1 us -> 0 us
  between operations: 14.1 us -> 0.02 us
  local copies, waits for them, and re-layouts: 17.4 us -> 6.21 us
    all_gather x2 -> x0, waiting for transfers between devices: 104 us -> none  [the longest x1 53 us: per_device(): full_out = lax.all_gather(w_out[0], DP, axis=0, tiled=True)]
    pallas_call x2 -> x1, Pallas kernels: 263 us -> 324 us  [per_device(): pl.pallas_call(step_kernel, out_shape=jax.ShapeDtypeStruct(block, BF16),...]
    all_gather x1 -> x0, blocking collectives: 25.7 us -> none  [per_device(): low = lax.all_gather(embedding.astype(BF16), DP, axis=0, tiled=True)]
    unnamed x1 -> x0, blocking collectives: 14.4 us -> none
    unnamed x12 -> x1, local copies, waits for them, and re-layouts: 15.6 us -> 2.51 us
  transfers between devices with their start and end apart: 2 -> 0, of which waited for: 2 -> 0; matrix products, arithmetic and copies ran while one was open for 3% -> 0% of each run, Pallas kernels for 0% -> 0%
where the time goes in v2:
time: 337 us; the launch traced here: 335 us
  Pallas kernels  324 us (96%)
  local copies, waits for them, and re-layouts  6.21 us (2%)
  other arithmetic  5.06 us (2%)
    pallas_call x1, Pallas kernels, per_device(): pl.pallas_call(step_kernel, out_shape=jax.ShapeDtypeStruct(block, BF16),...  324 us

profile of v2, /device:TPU:1, one launch (start us, length us, event | category | flops | bytes accessed | tf_op | source)
XLA Modules:
  0.0 335.1 jit_solution(13178338292406890890)
XLA Ops:
  0.0 0.7 convert_element_type.53
  0.7 0.1 broadcast_in_dim.11
  0.7 0.7 broadcast_add_fusion
  1.4 0.7 iota_compare_fusion.2
  2.1 0.7 convert_element_type.56.positive
  2.8 0.6 add_convert_fusion
  3.5 1.3 broadcast_in_dim.10.final_gain
  4.8 0.2 fusion.2
  5.0 0.7 pad_maximum_fusion
  5.7 0.7 fusion.1.last_mask
  6.4 0.7 fusion.spread_rows
  7.1 1.6 pad.4.wo_own
  8.8 323.8 %shard_map.73 = bf16[4,48,3584]{2,1,0:T(8,128)(2,1)} custom-call(bf16[4,48,3584]{2,1,0:T(8,128)(2,1)} %bitcast.6, f32[1,3584]{1,0:T(1,128)} %gain.1, bf16[112,1152]{1,0:T(8,128)(2,1)} %bitcast.7, bf16[32,3584]{1,0:T(8,128)(2,1)} %pad.4.wo_own, f32[48,128]{1,0:T(8,128)} %get-tuple-element.8.cosine, f32[48,128]{1,0:T(8,128)} %get-tuple-element.9.sine, ...), custom_call_target="tpu_custom_call" | custom-call | tf_op jit(solution)/shard_map/pallas_call | solution.py:546
  332.6 2.5 copy.10
  (3 shorter events, 0.0 us)

commit v3 on v2

--- a/solution.py
+++ b/solution.py
@@ -1,7 +1,6 @@
-import functools
-
 import jax
 import jax.numpy as jnp
+import numpy as np
 from jax import lax
 from jax.experimental import pallas as pl
 from jax.experimental.pallas import tpu as pltpu
@@ -71,11 +70,30 @@
     return chosen[0] if len(chosen) == 1 else jnp.concatenate(chosen, axis=0)
 
 
-def layer_forward(hidden, gain, wq, wo, cosine, sine, key_mask, roll):
-    wide = hidden.astype(F32)
-    inverse = lax.rsqrt(jnp.mean(wide * wide, axis=-1, keepdims=True) + norm_eps)
-    normed = (wide * inverse * gain).astype(BF16)
-    projected = nn(normed, wq[...])
+CHUNKS = ((0, 1024), (1024, 1024), (2048, 1024), (3072, 512))
+
+
+def live_lanes(shape, length):
+    lane = lanes_of(shape)
+    return jnp.where(lane < LENGTH, lane, lane - LENGTH) < length
+
+
+def is_last(length):
+    return lax.broadcasted_iota(jnp.int32, (LENGTH, 1), 0) == length - 1
+
+
+def project(chunk_of, gain, wq):
+    squares, projected = 0.0, 0.0
+    for low, size in CHUNKS:
+        wide = chunk_of(low, size).astype(F32)
+        squares = squares + jnp.sum(wide * wide, axis=-1, keepdims=True)
+        gained = (wide * gain[:, low : low + size]).astype(BF16)
+        projected = projected + nn(gained, wq[low : low + size, :])
+    inverse = lax.rsqrt(squares * (1.0 / 3584) + norm_eps)
+    return projected * inverse, inverse
+
+
+def attend(projected, length, cosine, sine, roll):
     blocks = [projected[:, 128 * b : 128 * (b + 1)] for b in range(9)]
     turned_blocks = [turned(b, cosine, sine, roll) for b in blocks[:8]]
     queries = [b.astype(BF16) for b in turned_blocks[:PAIRS]]
@@ -87,7 +105,7 @@
     context = []
     for span, key_form, value_form in zip(SPANS, key_forms, value_forms):
         scores = nt(stacked(queries, span), key_form) * HEAD_DIM ** (-0.5)
-        weights = jnp.where(key_mask > 0, jnp.exp(scores), 0.0)
+        weights = jnp.where(live_lanes(scores.shape, length), jnp.exp(scores), 0.0)
         low = lanes_of(weights.shape) < LENGTH
         sum_low = jnp.sum(jnp.where(low, weights, 0.0), axis=-1, keepdims=True)
         sum_high = jnp.sum(jnp.where(low, 0.0, weights), axis=-1, keepdims=True)
@@ -96,20 +114,22 @@
         result = nn(probability, value_form).astype(BF16)
         for i in range(span[1] - span[0]):
             context.append(result[LENGTH * i : LENGTH * (i + 1)])
-    branch = nn(jnp.concatenate(context, axis=1), wo[...])
-    following = (wide + branch).astype(BF16)
     saved = jnp.concatenate(queries + [keys, values], axis=1)
-    return following, saved, jnp.concatenate(probabilities, axis=0)
-
-
-def layer_backward(grad, hidden, saved, probabilities, gain, wq, wo, cosine, sine, roll):
+    return jnp.concatenate(context, axis=1), saved, jnp.concatenate(probabilities, axis=0)
+
+
+def context_gradient(chunk_of, wo):
+    total = 0.0
+    for low, size in CHUNKS:
+        total = total + nt(chunk_of(low, size), wo[:, low : low + size])
+    return total.astype(BF16)
+
+
+def attend_back(context_grad, saved, probabilities, cosine, sine, roll):
+    context_grads = [context_grad[:, 128 * b : 128 * (b + 1)] for b in range(PAIRS)]
     queries = [saved[:, 128 * b : 128 * (b + 1)] for b in range(PAIRS)]
     key_forms = paired(saved[:, 896:1024].astype(F32), roll)
     value_forms = paired(saved[:, 1024:1152].astype(F32), roll)
-    context_grad_t = nt(wo[...], grad)
-    context_grads = [
-        context_grad_t[128 * b : 128 * (b + 1)].T.astype(BF16) for b in range(PAIRS)
-    ]
     query_grads = []
     key_parts = []
     value_parts = []
@@ -137,19 +157,16 @@
         high_part = mixed[LENGTH:] + last[LENGTH:] + roll(last[:LENGTH], 64)
         return jnp.where(lanes_of(low_part.shape) < 64, low_part, high_part)
 
-    turned_back = [
-        turned(block.astype(BF16).astype(F32), cosine, -sine, roll).astype(BF16)
-        for block in query_grads + [folded(key_parts)]
+    grads = [
+        block.astype(BF16).astype(F32)
+        for block in query_grads + [folded(key_parts), folded(value_parts)]
     ]
-    projected_grad = jnp.concatenate(turned_back + [folded(value_parts).astype(BF16)], axis=1)
-    normed_grad = nt(wq[...], projected_grad).T
-    wide = hidden.astype(F32)
-    inverse = lax.rsqrt(jnp.mean(wide * wide, axis=-1, keepdims=True) + norm_eps)
-    gained = normed_grad * gain
-    inner = jnp.mean(gained * wide, axis=-1, keepdims=True)
-    return (
-        grad.astype(F32) + gained * inverse - wide * (inverse * inverse * inverse * inner)
-    ).astype(BF16)
+    product = 0.0
+    for b, block in enumerate(grads):
+        product = product + block * saved[:, 128 * b : 128 * (b + 1)].astype(F32)
+    turned_back = [turned(block, cosine, -sine, roll).astype(BF16) for block in grads[:8]]
+    projected_grad = jnp.concatenate(turned_back + [grads[8].astype(BF16)], axis=1)
+    return projected_grad, jnp.sum(product, axis=-1, keepdims=True)
 
 
 def tpu_roll(x, shift):
@@ -211,8 +228,8 @@
 
 
 class Gather:
-    def __init__(self, plane, own, whole, rows, cut, sends, receives, partner_receives):
-        self.plane, self.own, self.whole = plane, own, whole
+    def __init__(self, plane, whole, rows, cut, sends, receives, partner_receives):
+        self.plane, self.whole = plane, whole
         self.rows, self.cut = rows, cut
         self.sends, self.receives = sends, receives
         self.partner_receives = partner_receives
@@ -222,11 +239,11 @@
         low, size = ((0, self.rows), (0, self.cut), (self.cut, self.rows - self.cut))[half]
         return self.whole.at[pl.ds(pl.multiple_of(slot * self.rows + low, 16), size)]
 
-    def send(self, slot, half, place, receives=None, own=False):
+    def send(self, slot, half, place, receives=None):
         target = self.part(slot, half)
         receives = self.receives.at[slot // 2, max(half - 1, 0)] if receives is None else receives
         copy = remote(
-            self.own if own else target,
+            target,
             target,
             self.sends.at[len(self.started)],
             receives,
@@ -235,10 +252,8 @@
         copy.start()
         self.started.append(copy)
 
-    def hand_over(self, slot, own=False):
-        self.send(
-            slot, 0, self.plane.partner(), self.partner_receives.at[slot // 2], own=own
-        )
+    def hand_over(self, slot):
+        self.send(slot, 0, self.plane.partner(), self.partner_receives.at[slot // 2])
 
     def arrived(self, slot, half):
         part = self.part(slot, half)
@@ -251,19 +266,20 @@
         plane = self.plane
         slot = plane.slot(0, 0)
         for step in (1, -1):
-            self.send(slot, 0, plane.device(step, 0), own=True)
-            self.send(slot, 0, plane.device(0, step), own=True)
-        self.hand_over(slot, own=True)
-        self.whole[pl.ds(pl.multiple_of(slot * self.rows, 16), self.rows)] = self.own[...]
-
-    def first_ring(self):
+            self.send(slot, 0, plane.device(step, 0))
+            self.send(slot, 0, plane.device(0, step))
+        self.hand_over(slot)
+
+    def first_near(self):
         plane = self.plane
         for step, half in ((-1, 1), (1, 2)):
             slot = plane.slot(step, 0)
             self.arrived(slot, 0)
             self.send(slot, half, plane.device(-step, 0))
             self.spread(slot)
-        slot = plane.slot(2, 0)
+
+    def first_far(self):
+        slot = self.plane.slot(2, 0)
         self.arrived(slot, 1)
         self.arrived(slot, 2)
         self.spread(slot)
@@ -273,19 +289,19 @@
             self.send(slot, 0, self.plane.device(0, step))
         self.hand_over(slot)
 
-    def second_ring(self):
+    def second_near(self, first):
         plane = self.plane
-        for first in (0, -1, 1, 2):
-            for step, half in ((-1, 1), (1, 2)):
-                slot = plane.slot(first, step)
-                self.arrived(slot, 0)
-                self.send(slot, half, plane.device(0, -step))
-                self.hand_over(slot)
-        for first in (0, -1, 1, 2):
-            slot = plane.slot(first, 2)
-            self.arrived(slot, 1)
-            self.arrived(slot, 2)
+        for step, half in ((-1, 1), (1, 2)):
+            slot = plane.slot(first, step)
+            self.arrived(slot, 0)
+            self.send(slot, half, plane.device(0, -step))
             self.hand_over(slot)
+
+    def second_far(self, first):
+        slot = self.plane.slot(first, 2)
+        self.arrived(slot, 1)
+        self.arrived(slot, 2)
+        self.hand_over(slot)
 
     def from_partner(self):
         for at in range(16):
@@ -306,12 +322,13 @@
 def contrast(plane, last_rows, final_gain, positive, gathered, outgoing, sends, receives,
              partner_receives, last_grad):
     rows = jnp.concatenate([last_rows[m] for m in range(4)], axis=0)
-    gain = final_gain[...]
+    gain = final_gain[...].reshape(1, -1)
     inverse = lax.rsqrt(jnp.mean(rows * rows, axis=-1, keepdims=True) + norm_eps)
     pooled = rows * inverse * gain
     scale = lax.rsqrt(jnp.sum(pooled * pooled, axis=-1, keepdims=True))
     embedding = pooled * scale
-    tail = jnp.broadcast_to(positive[...], (4, 128))
+    spot = lax.broadcasted_iota(jnp.int32, (4, 128), 0)
+    tail = jnp.where(spot < 2, positive[0], positive[1]).astype(F32)
     packed = jnp.concatenate(
         [
             jnp.concatenate([embedding[:, 896 * k : 896 * (k + 1)], tail], axis=1)
@@ -394,29 +411,46 @@
 
 
 def step_kernel(
-    entry, gain, wq_own, wo_own, cosine, sine, key_mask, last_mask, final_gain, positive,
-    spread_rows,
+    lengths, positive, entry, gain, wq_own, wo_own, cosine, sine, final_gain, spread_rows,
     grad_out,
-    wq, wo_spaced, wo, hidden, saved, prob, last_rows, last_grad, embeds, embed_own,
-    inbox, outbox, back_inbox, back_outbox,
+    wq, wo_spaced, wo, hidden, saved, prob, inverses, last_rows, last_grad, embeds, embed_own,
+    outbox, grads,
     wq_send, wq_recv, wq_cross, wo_send, wo_recv, wo_cross, e_send, e_recv, e_cross,
-    f_send, f_recv, b_send, b_recv,
+    f_send, f_recv, b_send, b_recv, f_turn, b_turn,
 ):
     me = lax.axis_index("section")
     count = lax.axis_size("section")
     micros = entry.shape[0]
     plane = Plane()
+    mine = plane.slot(0, 0)
+    wq[pl.ds(pl.multiple_of(mine * 112, 16), 112)] = wq_own[...]
+    wo_spaced[pl.ds(pl.multiple_of(mine * 32, 16), 32)] = jnp.concatenate(
+        [wo_own[...], jnp.zeros((4, wo_own.shape[1]), BF16)], axis=0
+    )
     start_meeting(plane)
     gathers = (
-        Gather(plane, wq_own, wq, 112, 64, wq_send, wq_recv, wq_cross),
-        Gather(plane, wo_own, wo_spaced, 32, 16, wo_send, wo_recv, wo_cross),
+        Gather(plane, wq, 112, 64, wq_send, wq_recv, wq_cross),
+        Gather(plane, wo_spaced, 32, 16, wo_send, wo_recv, wo_cross),
     )
     for gather in gathers:
         gather.begin()
+
+    @pl.when(me == 0)
+    def _():
+        hidden[...] = entry[...]
+
     for gather in gathers:
-        gather.first_ring()
+        gather.first_near()
     for gather in gathers:
-        gather.second_ring()
+        gather.second_near(0)
+    for gather in gathers:
+        gather.first_far()
+    for first in (-1, 1, 2):
+        for gather in gathers:
+            gather.second_near(first)
+    for gather in gathers:
+        for first in (0, -1, 1, 2):
+            gather.second_far(first)
     for gather in gathers:
         gather.from_partner()
     for gather in gathers:
@@ -429,83 +463,129 @@
 
     lax.fori_loop(0, 4, pack, 0)
 
-    def hop(m):
+    def hop(m, k):
+        low, size = CHUNKS[k]
         return remote(
-            outbox.at[m], inbox.at[m], f_send.at[m], f_recv.at[m],
-            {"section": lax.rem(me + 1, count)},
-        )
+            outbox.at[m, :, pl.ds(low, size)], hidden.at[m, :, pl.ds(low, size)],
+            f_send.at[m, k], f_recv.at[m, k], {"section": lax.rem(me + 1, count)},
+        )
+
+    def back_hop(m, k):
+        low, size = CHUNKS[k]
+        return remote(
+            grad_out.at[m, :, pl.ds(low, size)], grads.at[m, :, pl.ds(low, size)],
+            b_send.at[m, k], b_recv.at[m, k], {"section": lax.rem(me + count - 1, count)},
+        )
+
+    def take_turn(first, turn, m):
+        @pl.when(jnp.logical_and(me == first, plane.core + m > 0))
+        def _():
+            pl.semaphore_wait(turn, 1)
+
+    def give_turn(first, turn, m, copies):
+        @pl.when(me == first)
+        def _():
+            for k in range(len(CHUNKS)):
+                copies(m, k).wait_send()
+
+        @pl.when(jnp.logical_and(me == first, m + plane.core < micros))
+        def _():
+            pl.semaphore_signal(
+                turn, inc=1, device_id=plane.partner(), device_id_type=pl.DeviceIdType.MESH
+            )
 
     def forward(m, carry):
-        @pl.when(me == 0)
-        def _():
-            hidden[m] = entry[m]
-
-        @pl.when(me > 0)
-        def _():
-            hop(m).wait_recv()
-            hidden[m] = inbox[m]
-
-        following, kept, probabilities = layer_forward(
-            hidden[m], gain[...], wq, wo, cosine[...], sine[...], key_mask[m], tpu_roll
-        )
-        outbox[m] = following
-
-        @pl.when(me < count - 1)
-        def _():
-            hop(m).start()
-
+        length = lengths[m]
+
+        def chunk_of(low, size):
+            k = [c[0] for c in CHUNKS].index(low)
+
+            @pl.when(me > 0)
+            def _():
+                hop(m, k).wait_recv()
+
+            return hidden[m, :, low : low + size]
+
+        projected, inverse = project(chunk_of, gain, wq)
+        inverses[m] = inverse
+        context, kept, probabilities = attend(
+            projected, length, cosine[...], sine[...], tpu_roll
+        )
+        last = is_last(length)
+        for k, (low, size) in enumerate(CHUNKS):
+            wide = hidden[m, :, low : low + size].astype(F32)
+            following = (wide + nn(context, wo[:, low : low + size])).astype(BF16)
+            outbox[m, :, low : low + size] = following
+            if k == 0:
+                take_turn(0, f_turn, m)
+
+            @pl.when(me < count - 1)
+            def _():
+                hop(m, k).start()
+
+            last_rows[m, :, low : low + size] = jnp.sum(
+                jnp.where(last, following.astype(F32), 0.0), axis=0, keepdims=True
+            )
         saved[m] = kept
         prob[m] = probabilities
-        last_rows[m] = jnp.sum(following.astype(F32) * last_mask[m], axis=0, keepdims=True)
+        give_turn(0, f_turn, m, hop)
         return carry
 
     lax.fori_loop(0, micros, forward, 0)
 
-    @pl.when(me < count - 1)
+    @pl.when(jnp.logical_and(me > 0, me < count - 1))
     def _():
         for m in range(micros):
-            hop(m).wait_send()
+            for k in range(len(CHUNKS)):
+                hop(m, k).wait_send()
 
     @pl.when(me == count - 1)
     def _():
         contrast(plane, last_rows, final_gain, positive, embeds, embed_own, e_send, e_recv,
                  e_cross, last_grad)
-
-    def back_hop(m):
-        return remote(
-            back_outbox.at[m], back_inbox.at[m], b_send.at[m], b_recv.at[m],
-            {"section": lax.rem(me + count - 1, count)},
-        )
+        for m in range(micros):
+            grads[m] = jnp.where(is_last(lengths[m]), last_grad[m], 0.0).astype(BF16)
 
     def backward(m, carry):
-        @pl.when(me == count - 1)
-        def _():
-            grad_out[m] = jnp.where(last_mask[m] > 0, last_grad[m], 0.0).astype(BF16)
-
-        @pl.when(me < count - 1)
-        def _():
-            back_hop(m).wait_recv()
-            grad_out[m] = back_inbox[m]
-
-        downstream = layer_backward(
-            grad_out[m], hidden[m], saved[m], prob[m],
-            gain[...], wq, wo, cosine[...], sine[...], tpu_roll,
-        )
-        back_outbox[m] = downstream
-
-        @pl.when(me > 0)
-        def _():
-            back_hop(m).start()
-
-        grad_out[m] = downstream
+        def chunk_of(low, size):
+            k = [c[0] for c in CHUNKS].index(low)
+
+            @pl.when(me < count - 1)
+            def _():
+                back_hop(m, k).wait_recv()
+
+            return grads[m, :, low : low + size]
+
+        context_grad = context_gradient(chunk_of, wo)
+        projected_grad, product = attend_back(
+            context_grad, saved[m], prob[m], cosine[...], sine[...], tpu_roll
+        )
+        inverse = inverses[m]
+        lean = inverse * inverse * product * (1.0 / 3584)
+        for k, (low, size) in enumerate(CHUNKS):
+            normed_grad = nt(projected_grad, wq[low : low + size, :])
+            grad_out[m, :, low : low + size] = (
+                grads[m, :, low : low + size].astype(F32)
+                + normed_grad * gain[:, low : low + size] * inverse
+                - hidden[m, :, low : low + size].astype(F32) * lean
+            ).astype(BF16)
+            if k == 0:
+                take_turn(count - 1, b_turn, m)
+
+            @pl.when(me > 0)
+            def _():
+                back_hop(m, k).start()
+
+        give_turn(count - 1, b_turn, m, back_hop)
         return carry
 
     lax.fori_loop(0, micros, backward, 0)
 
-    @pl.when(me > 0)
+    @pl.when(jnp.logical_and(me > 0, me < count - 1))
     def _():
         for m in range(micros):
-            back_hop(m).wait_send()
+            for k in range(len(CHUNKS)):
+                back_hop(m, k).wait_send()
 
 
 def whole():
@@ -514,12 +594,12 @@
 
 def turning(length):
     half = HEAD_DIM // 2
-    frequency = rope_base ** (-jnp.arange(half, dtype=F32) * (2.0 / HEAD_DIM))
-    angles = jnp.arange(length, dtype=jnp.int32).astype(F32)[:, None] * frequency[None, :]
-    cosine, sine = jnp.cos(angles), jnp.sin(angles)
+    frequency = rope_base ** (-np.arange(half, dtype=np.float32) * np.float32(2.0 / HEAD_DIM))
+    angles = np.arange(length, dtype=np.float32)[:, None] * frequency[None, :].astype(np.float32)
+    cosine, sine = np.cos(angles), np.sin(angles)
     return (
-        jnp.concatenate([cosine] * 4, axis=1),
-        jnp.concatenate([-sine, sine] * 2, axis=1),
+        np.concatenate([cosine] * 4, axis=1).astype(np.float32),
+        np.concatenate([-sine, sine] * 2, axis=1).astype(np.float32),
     )
 
 
@@ -528,25 +608,22 @@
     seqs = lengths.shape[0]
     length = entry.shape[0] // seqs
     cosine, sine = turning(length)
-    spots = jnp.arange(length, dtype=jnp.int32)
-    live = (spots[None, :] < lengths[:, None]).astype(F32)
-    key_mask = jnp.concatenate([live, live], axis=1)[:, None, :]
-    last_mask = (spots[None, :] == lengths[:, None] - 1).astype(F32)[:, :, None]
-    target = jnp.repeat(positive, 2).astype(F32)[:, None]
-    packed = jnp.arange(224)
-    spread_rows = (
-        jnp.arange(256)[None, :] == (packed // 28 * 32 + packed % 28)[:, None]
-    ).astype(BF16)
+    packed = np.arange(224)
+    spread_rows = np.arange(256)[None, :] == (packed // 28 * 32 + packed % 28)[:, None]
     block = (seqs, length, width)
     dma = pltpu.SemaphoreType.DMA
     args = (
-        entry.reshape(block), norm_gain, w_qkv[0], jnp.pad(w_out[0], ((0, 4), (0, 0))),
-        cosine, sine, key_mask, last_mask, final_gain[None, :], target, spread_rows,
-    )
+        lengths, positive,
+        entry.reshape(block), norm_gain, w_qkv[0], w_out[0],
+        jnp.asarray(cosine), jnp.asarray(sine), final_gain,
+        jnp.asarray(spread_rows.astype(np.float32), dtype=BF16),
+    )
+    small = pl.BlockSpec(memory_space=pltpu.SMEM)
+    chunks = len(CHUNKS)
     grads = pl.pallas_call(
         step_kernel,
         out_shape=jax.ShapeDtypeStruct(block, BF16),
-        in_specs=[whole()] * len(args),
+        in_specs=[small] * 2 + [whole()] * (len(args) - 2),
         out_specs=whole(),
         scratch_shapes=[
             pltpu.VMEM((width, 1152), BF16),
@@ -555,18 +632,18 @@
             pltpu.VMEM(block, BF16),
             pltpu.VMEM((seqs, length, 1152), BF16),
             pltpu.VMEM((seqs, PAIRS * length, 2 * length), BF16),
+            pltpu.VMEM((seqs, length, 1), F32),
             pltpu.VMEM((seqs, 1, width), F32),
             pltpu.VMEM((seqs, 1, width), F32),
             pltpu.VMEM((32, 16, 1024), BF16),
             pltpu.VMEM((16, 1024), BF16),
             pltpu.VMEM(block, BF16),
             pltpu.VMEM(block, BF16),
-            pltpu.VMEM(block, BF16),
-            pltpu.VMEM(block, BF16),
             dma((GATHER_SENDS,)), dma((16, 2)), dma((16,)),
             dma((GATHER_SENDS,)), dma((16, 2)), dma((16,)),
             dma((31,)), dma((16,)), dma((16,)),
-            dma((seqs,)), dma((seqs,)), dma((seqs,)), dma((seqs,)),
+            dma((seqs, chunks)), dma((seqs, chunks)), dma((seqs, chunks)), dma((seqs, chunks)),
+            pltpu.SemaphoreType.REGULAR, pltpu.SemaphoreType.REGULAR,
         ],
         compiler_params=pltpu.CompilerParams(
             collective_id=0, has_side_effects=True, vmem_limit_bytes=64000 * 1024

time: 337 us -> 278 us (0.82)
  Pallas kernels: 324 us -> 276 us
  other arithmetic: 5.06 us -> 0 us
  local copies, waits for them, and re-layouts: 6.21 us -> 2.51 us
    pallas_call x1, Pallas kernels: 324 us -> 276 us  [per_device(): pl.pallas_call(step_kernel, out_shape=jax.ShapeDtypeStruct(block, BF16),...]
where the time goes in v3:
time: 278 us
  Pallas kernels  276 us (99%)
    pallas_call x1, Pallas kernels, per_device(): pl.pallas_call(step_kernel, out_shape=jax.ShapeDtypeStruct(block, BF16),...  276 us

profile of v3, /device:TPU:1, one launch (start us, length us, event | category | flops | bytes accessed | tf_op | source)
XLA Modules:
  0.0 278.2 jit_solution(8490178874677815918)
XLA Ops:
  0.0 275.7 %shard_map.100 = bf16[4,48,3584]{2,1,0:T(8,128)(2,1)} custom-call(s32[4]{0:T(128)} %lengths.1, s32[2]{0:T(128)} %positive.1, bf16[4,48,3584]{2,1,0:T(8,128)(2,1)} %bitcast.5, f32[1,3584]{1,0:T(1,128)} %gain.1, bf16[112,1152]{1,0:T(8,128)(2,1)} %bitcast.6, bf16[28,3584]{1,0:T(8,128)(2,1)} %bitcast.7, f32[48,128]{1,0:T(8,128)} %constant.6.clone.cosine, ...), custom_call_target="tpu_custom_call" | custom-call | tf_op jit(solution)/shard_map/pallas_call | solution.py:623
  275.7 2.5 copy.12

commit v4 on v3

--- a/solution.py
+++ b/solution.py
@@ -70,7 +70,7 @@
     return chosen[0] if len(chosen) == 1 else jnp.concatenate(chosen, axis=0)
 
 
-CHUNKS = ((0, 1024), (1024, 1024), (2048, 1024), (3072, 512))
+CHUNKS = ((0, 512), (512, 1024), (1536, 1024), (2560, 512), (3072, 512))
 
 
 def live_lanes(shape, length):
@@ -109,7 +109,7 @@
         low = lanes_of(weights.shape) < LENGTH
         sum_low = jnp.sum(jnp.where(low, weights, 0.0), axis=-1, keepdims=True)
         sum_high = jnp.sum(jnp.where(low, 0.0, weights), axis=-1, keepdims=True)
-        probability = (weights / jnp.where(low, sum_low, sum_high)).astype(BF16)
+        probability = (weights * jnp.where(low, 1.0 / sum_low, 1.0 / sum_high)).astype(BF16)
         probabilities.append(probability)
         result = nn(probability, value_form).astype(BF16)
         for i in range(span[1] - span[0]):
@@ -185,16 +185,17 @@
 
 
 class Plane:
-    def __init__(self):
+    def __init__(self, flipped=False):
         self.x = lax.axis_index("dp_0")
         self.y = lax.axis_index("dp_1")
         self.core = lax.axis_index("dp_2")
+        self.turned = 1 - self.core if flipped else self.core
 
     def spot(self, first, second):
-        other = 1 - self.core
+        other = 1 - self.turned
         return (
-            lax.rem(self.x + first * other + second * self.core, 4),
-            lax.rem(self.y + first * self.core + second * other, 4),
+            lax.rem(self.x + first * other + second * self.turned, 4),
+            lax.rem(self.y + first * self.turned + second * other, 4),
         )
 
     def slot(self, first, second, mine=True):
@@ -224,7 +225,7 @@
         pl.semaphore_signal(
             barrier, inc=1, device_id=place, device_id_type=pl.DeviceIdType.MESH
         )
-    pl.semaphore_wait(barrier, len(places))
+    return barrier, len(places)
 
 
 class Gather:
@@ -303,8 +304,8 @@
         self.arrived(slot, 2)
         self.hand_over(slot)
 
-    def from_partner(self):
-        for at in range(16):
+    def from_partner(self, b):
+        for at in range(4 * b, 4 * b + 4):
             part = self.part(self.plane.partner_slot(at // 4, at % 4), 0)
             remote(
                 part, part, self.sends.at[0], self.partner_receives.at[at],
@@ -416,21 +417,22 @@
     wq, wo_spaced, wo, hidden, saved, prob, inverses, last_rows, last_grad, embeds, embed_own,
     outbox, grads,
     wq_send, wq_recv, wq_cross, wo_send, wo_recv, wo_cross, e_send, e_recv, e_cross,
-    f_send, f_recv, b_send, b_recv, f_turn, b_turn,
+    f_send, f_recv, b_send, b_recv,
 ):
     me = lax.axis_index("section")
     count = lax.axis_size("section")
     micros = entry.shape[0]
     plane = Plane()
     mine = plane.slot(0, 0)
+    barrier, greetings = start_meeting(plane)
     wq[pl.ds(pl.multiple_of(mine * 112, 16), 112)] = wq_own[...]
     wo_spaced[pl.ds(pl.multiple_of(mine * 32, 16), 32)] = jnp.concatenate(
         [wo_own[...], jnp.zeros((4, wo_own.shape[1]), BF16)], axis=0
     )
-    start_meeting(plane)
+    pl.semaphore_wait(barrier, greetings)
     gathers = (
         Gather(plane, wq, 112, 64, wq_send, wq_recv, wq_cross),
-        Gather(plane, wo_spaced, 32, 16, wo_send, wo_recv, wo_cross),
+        Gather(Plane(flipped=True), wo_spaced, 32, 16, wo_send, wo_recv, wo_cross),
     )
     for gather in gathers:
         gather.begin()
@@ -451,17 +453,14 @@
     for gather in gathers:
         for first in (0, -1, 1, 2):
             gather.second_far(first)
-    for gather in gathers:
-        gather.from_partner()
+    for b in range(4):
+        gathers[1].from_partner(b)
+        spaced = wo_spaced[256 * b : 256 * (b + 1)]
+        wo[224 * b : 224 * (b + 1)] = nn(spread_rows[...], spaced).astype(BF16)
+    for b in range(4):
+        gathers[0].from_partner(b)
     for gather in gathers:
         gather.drain()
-
-    def pack(b, carry):
-        spaced = wo_spaced[pl.ds(pl.multiple_of(b * 256, 256), 256)]
-        wo[pl.ds(pl.multiple_of(b * 224, 16), 224)] = nn(spread_rows[...], spaced).astype(BF16)
-        return carry
-
-    lax.fori_loop(0, 4, pack, 0)
 
     def hop(m, k):
         low, size = CHUNKS[k]
@@ -477,23 +476,6 @@
             b_send.at[m, k], b_recv.at[m, k], {"section": lax.rem(me + count - 1, count)},
         )
 
-    def take_turn(first, turn, m):
-        @pl.when(jnp.logical_and(me == first, plane.core + m > 0))
-        def _():
-            pl.semaphore_wait(turn, 1)
-
-    def give_turn(first, turn, m, copies):
-        @pl.when(me == first)
-        def _():
-            for k in range(len(CHUNKS)):
-                copies(m, k).wait_send()
-
-        @pl.when(jnp.logical_and(me == first, m + plane.core < micros))
-        def _():
-            pl.semaphore_signal(
-                turn, inc=1, device_id=plane.partner(), device_id_type=pl.DeviceIdType.MESH
-            )
-
     def forward(m, carry):
         length = lengths[m]
 
@@ -516,8 +498,6 @@
             wide = hidden[m, :, low : low + size].astype(F32)
             following = (wide + nn(context, wo[:, low : low + size])).astype(BF16)
             outbox[m, :, low : low + size] = following
-            if k == 0:
-                take_turn(0, f_turn, m)
 
             @pl.when(me < count - 1)
             def _():
@@ -528,12 +508,11 @@
             )
         saved[m] = kept
         prob[m] = probabilities
-        give_turn(0, f_turn, m, hop)
         return carry
 
     lax.fori_loop(0, micros, forward, 0)
 
-    @pl.when(jnp.logical_and(me > 0, me < count - 1))
+    @pl.when(me < count - 1)
     def _():
         for m in range(micros):
             for k in range(len(CHUNKS)):
@@ -569,19 +548,16 @@
                 + normed_grad * gain[:, low : low + size] * inverse
                 - hidden[m, :, low : low + size].astype(F32) * lean
             ).astype(BF16)
-            if k == 0:
-                take_turn(count - 1, b_turn, m)
 
             @pl.when(me > 0)
             def _():
                 back_hop(m, k).start()
 
-        give_turn(count - 1, b_turn, m, back_hop)
         return carry
 
     lax.fori_loop(0, micros, backward, 0)
 
-    @pl.when(jnp.logical_and(me > 0, me < count - 1))
+    @pl.when(me > 0)
     def _():
         for m in range(micros):
             for k in range(len(CHUNKS)):
@@ -643,7 +619,6 @@
             dma((GATHER_SENDS,)), dma((16, 2)), dma((16,)),
             dma((31,)), dma((16,)), dma((16,)),
             dma((seqs, chunks)), dma((seqs, chunks)), dma((seqs, chunks)), dma((seqs, chunks)),
-            pltpu.SemaphoreType.REGULAR, pltpu.SemaphoreType.REGULAR,
         ],
         compiler_params=pltpu.CompilerParams(
             collective_id=0, has_side_effects=True, vmem_limit_bytes=64000 * 1024

time: 278 us -> 270 us (0.971)
  Pallas kernels: 276 us -> 267 us
    pallas_call x1, Pallas kernels: 276 us -> 267 us  [per_device(): pl.pallas_call(step_kernel, out_shape=jax.ShapeDtypeStruct(block, BF16),...]
where the time goes in v4:
time: 270 us
  Pallas kernels  267 us (99%)
    pallas_call x1, Pallas kernels, per_device(): pl.pallas_call(step_kernel, out_shape=jax.ShapeDtypeStruct(block, BF16),...  267 us

profile of v4, /device:TPU:1, one launch (start us, length us, event | category | flops | bytes accessed | tf_op | source)
XLA Modules:
  0.0 269.7 jit_solution(2102130826007823591)
XLA Ops:
  0.0 267.2 %shard_map.100 = bf16[4,48,3584]{2,1,0:T(8,128)(2,1)} custom-call(s32[4]{0:T(128)} %lengths.1, s32[2]{0:T(128)} %positive.1, bf16[4,48,3584]{2,1,0:T(8,128)(2,1)} %bitcast.5, f32[1,3584]{1,0:T(1,128)} %gain.1, bf16[112,1152]{1,0:T(8,128)(2,1)} %bitcast.6, bf16[28,3584]{1,0:T(8,128)(2,1)} %bitcast.7, f32[48,128]{1,0:T(8,128)} %constant.6.clone.cosine, ...), custom_call_target="tpu_custom_call" | custom-call | tf_op jit(solution)/shard_map/pallas_call | solution.py:599
  267.2 2.5 copy.12

commit v5 on v4

--- a/solution.py
+++ b/solution.py
@@ -18,6 +18,7 @@
 objective_coefficient = 256.0
 
 LENGTH = 48
+EARLY = 2
 PAIRS = 7
 F32 = jnp.float32
 BF16 = jnp.bfloat16
@@ -70,7 +71,8 @@
     return chosen[0] if len(chosen) == 1 else jnp.concatenate(chosen, axis=0)
 
 
-CHUNKS = ((0, 512), (512, 1024), (1536, 1024), (2560, 512), (3072, 512))
+CHUNKS = ((0, 512), (512, 2048), (2560, 1024))
+BACK_CHUNKS = ((0, 512), (512, 1024), (1536, 1280), (2816, 768))
 
 
 def live_lanes(shape, length):
@@ -120,7 +122,7 @@
 
 def context_gradient(chunk_of, wo):
     total = 0.0
-    for low, size in CHUNKS:
+    for low, size in BACK_CHUNKS:
         total = total + nt(chunk_of(low, size), wo[:, low : low + size])
     return total.astype(BF16)
 
@@ -363,9 +365,6 @@
         remote(
             outgoing, gathered.at[slot], sends.at[0], partner_receives.at[at], plane.partner()
         ).wait_recv()
-    for copy in started:
-        copy.wait_send()
-
     flat = jnp.concatenate([gathered[i] for i in range(32)], axis=0)
     at = lax.broadcasted_iota(jnp.int32, (128, 512), 0)
     lane = lanes_of((128, 512))
@@ -409,6 +408,8 @@
     )
     for m in range(4):
         last_grad[m] = row_grad[m : m + 1]
+    for copy in started:
+        copy.wait_send()
 
 
 def step_kernel(
@@ -417,7 +418,7 @@
     wq, wo_spaced, wo, hidden, saved, prob, inverses, last_rows, last_grad, embeds, embed_own,
     outbox, grads,
     wq_send, wq_recv, wq_cross, wo_send, wo_recv, wo_cross, e_send, e_recv, e_cross,
-    f_send, f_recv, b_send, b_recv,
+    f_send, f_recv, b_send, b_recv, f_turn, b_turn,
 ):
     me = lax.axis_index("section")
     count = lax.axis_size("section")
@@ -470,11 +471,28 @@
         )
 
     def back_hop(m, k):
-        low, size = CHUNKS[k]
+        low, size = BACK_CHUNKS[k]
         return remote(
             grad_out.at[m, :, pl.ds(low, size)], grads.at[m, :, pl.ds(low, size)],
             b_send.at[m, k], b_recv.at[m, k], {"section": lax.rem(me + count - 1, count)},
         )
+
+    def take_turn(sending, turn, m):
+        @pl.when(jnp.logical_and(sending, plane.core + m > 0))
+        def _():
+            pl.semaphore_wait(turn, 1)
+
+    def give_turn(sending, turn, m, copies):
+        @pl.when(sending)
+        def _():
+            for k in range(EARLY):
+                copies(m, k).wait_send()
+
+        @pl.when(jnp.logical_and(sending, m + plane.core < micros))
+        def _():
+            pl.semaphore_signal(
+                turn, inc=1, device_id=plane.partner(), device_id_type=pl.DeviceIdType.MESH
+            )
 
     def forward(m, carry):
         length = lengths[m]
@@ -498,6 +516,8 @@
             wide = hidden[m, :, low : low + size].astype(F32)
             following = (wide + nn(context, wo[:, low : low + size])).astype(BF16)
             outbox[m, :, low : low + size] = following
+            if k == 0:
+                take_turn(me < count - 1, f_turn, m)
 
             @pl.when(me < count - 1)
             def _():
@@ -508,6 +528,7 @@
             )
         saved[m] = kept
         prob[m] = probabilities
+        give_turn(me < count - 1, f_turn, m, hop)
         return carry
 
     lax.fori_loop(0, micros, forward, 0)
@@ -515,7 +536,7 @@
     @pl.when(me < count - 1)
     def _():
         for m in range(micros):
-            for k in range(len(CHUNKS)):
+            for k in range(EARLY, len(CHUNKS)):
                 hop(m, k).wait_send()
 
     @pl.when(me == count - 1)
@@ -527,7 +548,7 @@
 
     def backward(m, carry):
         def chunk_of(low, size):
-            k = [c[0] for c in CHUNKS].index(low)
+            k = [c[0] for c in BACK_CHUNKS].index(low)
 
             @pl.when(me < count - 1)
             def _():
@@ -541,18 +562,21 @@
         )
         inverse = inverses[m]
         lean = inverse * inverse * product * (1.0 / 3584)
-        for k, (low, size) in enumerate(CHUNKS):
+        for k, (low, size) in enumerate(BACK_CHUNKS):
             normed_grad = nt(projected_grad, wq[low : low + size, :])
             grad_out[m, :, low : low + size] = (
                 grads[m, :, low : low + size].astype(F32)
                 + normed_grad * gain[:, low : low + size] * inverse
                 - hidden[m, :, low : low + size].astype(F32) * lean
             ).astype(BF16)
+            if k == 0:
+                take_turn(me > 0, b_turn, m)
 
             @pl.when(me > 0)
             def _():
                 back_hop(m, k).start()
 
+        give_turn(me > 0, b_turn, m, back_hop)
         return carry
 
     lax.fori_loop(0, micros, backward, 0)
@@ -560,7 +584,7 @@
     @pl.when(me > 0)
     def _():
         for m in range(micros):
-            for k in range(len(CHUNKS)):
+            for k in range(EARLY, len(BACK_CHUNKS)):
                 back_hop(m, k).wait_send()
 
 
@@ -595,7 +619,7 @@
         jnp.asarray(spread_rows.astype(np.float32), dtype=BF16),
     )
     small = pl.BlockSpec(memory_space=pltpu.SMEM)
-    chunks = len(CHUNKS)
+    chunks, back_chunks = len(CHUNKS), len(BACK_CHUNKS)
     grads = pl.pallas_call(
         step_kernel,
         out_shape=jax.ShapeDtypeStruct(block, BF16),
@@ -618,7 +642,9 @@
             dma((GATHER_SENDS,)), dma((16, 2)), dma((16,)),
             dma((GATHER_SENDS,)), dma((16, 2)), dma((16,)),
             dma((31,)), dma((16,)), dma((16,)),
-            dma((seqs, chunks)), dma((seqs, chunks)), dma((seqs, chunks)), dma((seqs, chunks)),
+            dma((seqs, chunks)), dma((seqs, chunks)),
+            dma((seqs, back_chunks)), dma((seqs, back_chunks)),
+            pltpu.SemaphoreType.REGULAR, pltpu.SemaphoreType.REGULAR,
         ],
         compiler_params=pltpu.CompilerParams(
             collective_id=0, has_side_effects=True, vmem_limit_bytes=64000 * 1024

time: 270 us -> 259 us (0.959)
  Pallas kernels: 267 us -> 257 us
    pallas_call x1, Pallas kernels: 267 us -> 257 us  [per_device(): pl.pallas_call(step_kernel, out_shape=jax.ShapeDtypeStruct(block, BF16),...]
where the time goes in v5:
time: 259 us
  Pallas kernels  257 us (99%)
    pallas_call x1, Pallas kernels, per_device(): pl.pallas_call(step_kernel, out_shape=jax.ShapeDtypeStruct(block, BF16),...  257 us

profile of v5, /device:TPU:1, one launch (start us, length us, event | category | flops | bytes accessed | tf_op | source)
XLA Modules:
  0.0 259.1 jit_solution(10117358747953805608)
XLA Ops:
  0.0 256.6 %shard_map.100 = bf16[4,48,3584]{2,1,0:T(8,128)(2,1)} custom-call(s32[4]{0:T(128)} %lengths.1, s32[2]{0:T(128)} %positive.1, bf16[4,48,3584]{2,1,0:T(8,128)(2,1)} %bitcast.5, f32[1,3584]{1,0:T(1,128)} %gain.1, bf16[112,1152]{1,0:T(8,128)(2,1)} %bitcast.6, bf16[28,3584]{1,0:T(8,128)(2,1)} %bitcast.7, f32[48,128]{1,0:T(8,128)} %constant.6.clone.cosine, ...), custom_call_target="tpu_custom_call" | custom-call | tf_op jit(solution)/shard_map/pallas_call | solution.py:623
  256.6 2.5 copy.12

commit v6 on v5

--- a/solution.py
+++ b/solution.py
@@ -111,7 +111,7 @@
         low = lanes_of(weights.shape) < LENGTH
         sum_low = jnp.sum(jnp.where(low, weights, 0.0), axis=-1, keepdims=True)
         sum_high = jnp.sum(jnp.where(low, 0.0, weights), axis=-1, keepdims=True)
-        probability = (weights * jnp.where(low, 1.0 / sum_low, 1.0 / sum_high)).astype(BF16)
+        probability = (weights / jnp.where(low, sum_low, sum_high)).astype(BF16)
         probabilities.append(probability)
         result = nn(probability, value_form).astype(BF16)
         for i in range(span[1] - span[0]):
@@ -127,11 +127,17 @@
     return total.astype(BF16)
 
 
-def attend_back(context_grad, saved, probabilities, cosine, sine, roll):
+def forms_of(saved, roll):
+    return (
+        paired(saved[:, 896:1024].astype(F32), roll),
+        paired(saved[:, 1024:1152].astype(F32), roll),
+    )
+
+
+def attend_back(context_grad, saved, forms, probabilities, cosine, sine, roll):
     context_grads = [context_grad[:, 128 * b : 128 * (b + 1)] for b in range(PAIRS)]
     queries = [saved[:, 128 * b : 128 * (b + 1)] for b in range(PAIRS)]
-    key_forms = paired(saved[:, 896:1024].astype(F32), roll)
-    value_forms = paired(saved[:, 1024:1152].astype(F32), roll)
+    key_forms, value_forms = forms
     query_grads = []
     key_parts = []
     value_parts = []
@@ -222,7 +228,7 @@
     barrier = pltpu.get_barrier_semaphore()
     places = [{"section": lax.rem(me + step, count)} for step in (1, count - 1)]
     places.append(plane.partner())
-    places += [plane.device(a, b) for a in range(4) for b in range(4) if a or b]
+    places += [plane.device(a, b) for a, b in ((1, 0), (3, 0), (0, 1), (0, 3))]
     for place in places:
         pl.semaphore_signal(
             barrier, inc=1, device_id=place, device_id_type=pl.DeviceIdType.MESH
@@ -354,6 +360,11 @@
     for a, b in reversed(others):
         send(outgoing, mine, receives.at[mine // 2], plane.device(a, b))
     send(outgoing, mine, partner_receives.at[mine // 2], plane.partner())
+    at = lax.broadcasted_iota(jnp.int32, (128, 512), 0)
+    lane = lanes_of((128, 512))
+    number = at & 63
+    row = (number >> 1) * 16 + (number & 1) * 2 + (at >> 6)
+    selections = [jnp.where(lane == row + 4 * k, 1.0, 0.0).astype(BF16) for k in range(4)]
     for a, b in others:
         slot = plane.slot(a, b)
         remote(
@@ -366,14 +377,7 @@
             outgoing, gathered.at[slot], sends.at[0], partner_receives.at[at], plane.partner()
         ).wait_recv()
     flat = jnp.concatenate([gathered[i] for i in range(32)], axis=0)
-    at = lax.broadcasted_iota(jnp.int32, (128, 512), 0)
-    lane = lanes_of((128, 512))
-    number = at & 63
-    row = (number >> 1) * 16 + (number & 1) * 2 + (at >> 6)
-    pieces = []
-    for k in range(4):
-        chosen = jnp.where(lane == row + 4 * k, 1.0, 0.0).astype(BF16)
-        pieces.append(nn(chosen, flat))
+    pieces = [nn(chosen, flat) for chosen in selections]
     everyone = jnp.concatenate([p[:, :896] for p in pieces], axis=1).astype(BF16)
     target = pieces[0][:64, 896:960]
     logits = nt(everyone[:64], everyone[64:]) * (1.0 / sharpness_divisor)
@@ -398,7 +402,8 @@
     rest = exact - top.astype(F32)
     middle = rest.astype(BF16)
     low = (rest - middle.astype(F32)).astype(BF16)
-    embed_grad = nn(top, everyone) + nn(middle, everyone) + nn(low, everyone)
+    parts = nn(jnp.concatenate([top, middle, low], axis=0), everyone)
+    embed_grad = parts[0:4] + parts[4:8] + parts[8:12]
     pooled_grad = embed_grad * scale - pooled * (
         scale * scale * scale * jnp.sum(embed_grad * pooled, axis=-1, keepdims=True)
     )
@@ -413,12 +418,12 @@
 
 
 def step_kernel(
-    lengths, positive, entry, gain, wq_own, wo_own, cosine, sine, final_gain, spread_rows,
+    lengths, positive, entry, gain, wq_own, wo_own, cosine, sine, final_gain,
     grad_out,
     wq, wo_spaced, wo, hidden, saved, prob, inverses, last_rows, last_grad, embeds, embed_own,
     outbox, grads,
     wq_send, wq_recv, wq_cross, wo_send, wo_recv, wo_cross, e_send, e_recv, e_cross,
-    f_send, f_recv, b_send, b_recv, f_turn, b_turn,
+    f_send, f_recv, b_send, b_recv, f_turn, b_turn, entry_sem,
 ):
     me = lax.axis_index("section")
     count = lax.axis_size("section")
@@ -440,7 +445,9 @@
 
     @pl.when(me == 0)
     def _():
-        hidden[...] = entry[...]
+        copy = pltpu.make_async_copy(entry, hidden, entry_sem)
+        copy.start()
+        copy.wait()
 
     for gather in gathers:
         gather.first_near()
@@ -456,8 +463,9 @@
             gather.second_far(first)
     for b in range(4):
         gathers[1].from_partner(b)
-        spaced = wo_spaced[256 * b : 256 * (b + 1)]
-        wo[224 * b : 224 * (b + 1)] = nn(spread_rows[...], spaced).astype(BF16)
+        wo[224 * b : 224 * (b + 1)] = jnp.concatenate(
+            [wo_spaced[256 * b + 32 * i : 256 * b + 32 * i + 28] for i in range(8)], axis=0
+        )
     for b in range(4):
         gathers[0].from_partner(b)
     for gather in gathers:
@@ -543,10 +551,14 @@
     def _():
         contrast(plane, last_rows, final_gain, positive, embeds, embed_own, e_send, e_recv,
                  e_cross, last_grad)
-        for m in range(micros):
-            grads[m] = jnp.where(is_last(lengths[m]), last_grad[m], 0.0).astype(BF16)
 
     def backward(m, carry):
+        length = lengths[m]
+
+        @pl.when(me == count - 1)
+        def _():
+            grads[m] = jnp.where(is_last(length), last_grad[m], 0.0).astype(BF16)
+
         def chunk_of(low, size):
             k = [c[0] for c in BACK_CHUNKS].index(low)
 
@@ -556,9 +568,10 @@
 
             return grads[m, :, low : low + size]
 
+        forms = forms_of(saved[m], tpu_roll)
         context_grad = context_gradient(chunk_of, wo)
         projected_grad, product = attend_back(
-            context_grad, saved[m], prob[m], cosine[...], sine[...], tpu_roll
+            context_grad, saved[m], forms, prob[m], cosine[...], sine[...], tpu_roll
         )
         inverse = inverses[m]
         lean = inverse * inverse * product * (1.0 / 3584)
@@ -603,27 +616,43 @@
     )
 
 
+def handed_on(source, target, held, come, go):
+    pieces = held.shape[0]
+    copies_in = [
+        pltpu.make_async_copy(source.at[i], held.at[i], come.at[i]) for i in range(pieces)
+    ]
+    copies_out = [
+        pltpu.make_async_copy(held.at[i], target.at[i], go.at[i]) for i in range(pieces)
+    ]
+    for copy in copies_in:
+        copy.start()
+    for coming, going in zip(copies_in, copies_out):
+        coming.wait()
+        going.start()
+    for copy in copies_out:
+        copy.wait()
+
+
 def per_device(entry, norm_gain, w_qkv, w_out, final_gain, lengths, positive):
     width = entry.shape[1]
     seqs = lengths.shape[0]
     length = entry.shape[0] // seqs
     cosine, sine = turning(length)
-    packed = np.arange(224)
-    spread_rows = np.arange(256)[None, :] == (packed // 28 * 32 + packed % 28)[:, None]
     block = (seqs, length, width)
     dma = pltpu.SemaphoreType.DMA
     args = (
         lengths, positive,
         entry.reshape(block), norm_gain, w_qkv[0], w_out[0],
         jnp.asarray(cosine), jnp.asarray(sine), final_gain,
-        jnp.asarray(spread_rows.astype(np.float32), dtype=BF16),
     )
     small = pl.BlockSpec(memory_space=pltpu.SMEM)
     chunks, back_chunks = len(CHUNKS), len(BACK_CHUNKS)
     grads = pl.pallas_call(
         step_kernel,
         out_shape=jax.ShapeDtypeStruct(block, BF16),
-        in_specs=[small] * 2 + [whole()] * (len(args) - 2),
+        in_specs=[small] * 2
+        + [pl.BlockSpec(memory_space=pl.ANY)]
+        + [whole()] * (len(args) - 3),
         out_specs=whole(),
         scratch_shapes=[
             pltpu.VMEM((width, 1152), BF16),
@@ -644,13 +673,20 @@
             dma((31,)), dma((16,)), dma((16,)),
             dma((seqs, chunks)), dma((seqs, chunks)),
             dma((seqs, back_chunks)), dma((seqs, back_chunks)),
-            pltpu.SemaphoreType.REGULAR, pltpu.SemaphoreType.REGULAR,
+            pltpu.SemaphoreType.REGULAR, pltpu.SemaphoreType.REGULAR, dma,
         ],
         compiler_params=pltpu.CompilerParams(
             collective_id=0, has_side_effects=True, vmem_limit_bytes=64000 * 1024
         ),
     )(*args)
-    return grads.reshape(1, seqs * length, width)
+    result = pl.pallas_call(
+        handed_on,
+        out_shape=jax.ShapeDtypeStruct(block, BF16),
+        in_specs=[pl.BlockSpec(memory_space=pl.ANY)],
+        out_specs=pl.BlockSpec(memory_space=pl.ANY),
+        scratch_shapes=[pltpu.VMEM(block, BF16), dma((seqs,)), dma((seqs,))],
+    )(grads)
+    return result.reshape(1, seqs * length, width)
 
 
 def solution(mesh):

time: 259 us -> 256 us (0.988)
    pallas_call x1, Pallas kernels: 257 us -> 254 us  [per_device(): pl.pallas_call(step_kernel, out_shape=jax.ShapeDtypeStruct(block, BF16),...]
where the time goes in v6:
time: 256 us
  Pallas kernels  256 us (100%)
    pallas_call x1, Pallas kernels, per_device(): pl.pallas_call(step_kernel, out_shape=jax.ShapeDtypeStruct(block, BF16),...  254 us

profile of v6, /device:TPU:1, one launch (start us, length us, event | category | flops | bytes accessed | tf_op | source)
XLA Modules:
  0.0 255.7 jit_solution(3251937384333278235)
XLA Ops:
  0.0 253.5 %shard_map.91.source = bf16[4,48,3584]{2,1,0:T(8,128)(2,1)} custom-call(s32[4]{0:T(128)} %lengths.1, s32[2]{0:T(128)} %positive.1, bf16[4,48,3584]{2,1,0:T(8,128)(2,1)} %bitcast.4, f32[1,3584]{1,0:T(1,128)} %gain.1, bf16[112,1152]{1,0:T(8,128)(2,1)} %bitcast.5, bf16[28,3584]{1,0:T(8,128)(2,1)} %bitcast.6, f32[48,128]{1,0:T(8,128)} %constant.4.clone.cosine, ...), custom_call_target="tpu_custom_call" | custom-call | tf_op jit(solution)/shard_map/pallas_call | solution.py:650
  253.5 2.1 shard_map.92

commit v7 on v6

--- a/solution.py
+++ b/solution.py
@@ -420,7 +420,7 @@
 def step_kernel(
     lengths, positive, entry, gain, wq_own, wo_own, cosine, sine, final_gain,
     grad_out,
-    wq, wo_spaced, wo, hidden, saved, prob, inverses, last_rows, last_grad, embeds, embed_own,
+    wq, wo_folded, wo, hidden, saved, prob, inverses, last_rows, last_grad, embeds, embed_own,
     outbox, grads,
     wq_send, wq_recv, wq_cross, wo_send, wo_recv, wo_cross, e_send, e_recv, e_cross,
     f_send, f_recv, b_send, b_recv, f_turn, b_turn, entry_sem,
@@ -432,13 +432,13 @@
     mine = plane.slot(0, 0)
     barrier, greetings = start_meeting(plane)
     wq[pl.ds(pl.multiple_of(mine * 112, 16), 112)] = wq_own[...]
-    wo_spaced[pl.ds(pl.multiple_of(mine * 32, 16), 32)] = jnp.concatenate(
-        [wo_own[...], jnp.zeros((4, wo_own.shape[1]), BF16)], axis=0
+    wo_folded[pl.ds(pl.multiple_of(mine * 112, 16), 112)] = jnp.concatenate(
+        [wo_own[:, 896 * k : 896 * (k + 1)] for k in range(4)], axis=0
     )
     pl.semaphore_wait(barrier, greetings)
     gathers = (
         Gather(plane, wq, 112, 64, wq_send, wq_recv, wq_cross),
-        Gather(Plane(flipped=True), wo_spaced, 32, 16, wo_send, wo_recv, wo_cross),
+        Gather(Plane(flipped=True), wo_folded, 112, 64, wo_send, wo_recv, wo_cross),
     )
     for gather in gathers:
         gather.begin()
@@ -463,9 +463,14 @@
             gather.second_far(first)
     for b in range(4):
         gathers[1].from_partner(b)
-        wo[224 * b : 224 * (b + 1)] = jnp.concatenate(
-            [wo_spaced[256 * b + 32 * i : 256 * b + 32 * i + 28] for i in range(8)], axis=0
-        )
+        for k in range(4):
+            wo[224 * b : 224 * (b + 1), 896 * k : 896 * (k + 1)] = jnp.concatenate(
+                [
+                    wo_folded[112 * i + 28 * k : 112 * i + 28 * (k + 1)]
+                    for i in range(8 * b, 8 * (b + 1))
+                ],
+                axis=0,
+            )
     for b in range(4):
         gathers[0].from_partner(b)
     for gather in gathers:
@@ -656,7 +661,7 @@
         out_specs=whole(),
         scratch_shapes=[
             pltpu.VMEM((width, 1152), BF16),
-            pltpu.VMEM((1024, width), BF16),
+            pltpu.VMEM((3584, 896), BF16),
             pltpu.VMEM((896, width), BF16),
             pltpu.VMEM(block, BF16),
             pltpu.VMEM((seqs, length, 1152), BF16),

time: 256 us -> 254 us (level)
  no operation moved by 1% of the time
where the time goes in v7:
time: 254 us
  Pallas kernels  254 us (100%)
    pallas_call x1, Pallas kernels, per_device(): pl.pallas_call(step_kernel, out_shape=jax.ShapeDtypeStruct(block, BF16),...  252 us

profile of v7, /device:TPU:1, one launch (start us, length us, event | category | flops | bytes accessed | tf_op | source)
XLA Modules:
  0.0 253.9 jit_solution(10791141958214770084)
XLA Ops:
  0.0 251.8 %shard_map.91.source = bf16[4,48,3584]{2,1,0:T(8,128)(2,1)} custom-call(s32[4]{0:T(128)} %lengths.1, s32[2]{0:T(128)} %positive.1, bf16[4,48,3584]{2,1,0:T(8,128)(2,1)} %bitcast.4, f32[1,3584]{1,0:T(1,128)} %gain.1, bf16[112,1152]{1,0:T(8,128)(2,1)} %bitcast.5, bf16[28,3584]{1,0:T(8,128)(2,1)} %bitcast.6, f32[48,128]{1,0:T(8,128)} %constant.4.clone.cosine, ...), custom_call_target="tpu_custom_call" | custom-call | tf_op jit(solution)/shard_map/pallas_call | solution.py:655
  251.8 2.1 shard_map.92

commit v8 on v7

--- a/solution.py
+++ b/solution.py
@@ -328,73 +328,120 @@
 GATHER_SENDS = 36
 
 
-def contrast(plane, last_rows, final_gain, positive, gathered, outgoing, sends, receives,
-             partner_receives, last_grad):
+class Exchange:
+    def __init__(self, plane, pair, gathered, outgoing, sends, receives, partner_receives):
+        self.plane, self.pair = plane, pair
+        self.gathered, self.outgoing = gathered.at[pair], outgoing.at[pair]
+        self.sends, self.receives = sends.at[pair], receives.at[pair]
+        self.partner_receives = partner_receives.at[pair]
+        others = [(a, b) for a in range(4) for b in range(4) if a or b]
+        others.sort(key=lambda ab: min(ab[0], 4 - ab[0]) + min(ab[1], 4 - ab[1]))
+        self.others = others
+
+    def copy(self, source, slot, at, receive, place):
+        return remote(source, self.gathered.at[slot], self.sends.at[at], receive, place)
+
+    def own_copies(self):
+        plane, mine = self.plane, self.plane.slot(0, 0)
+        found = [
+            self.copy(self.outgoing, mine, at, self.receives.at[mine // 2], plane.device(*place))
+            for at, place in enumerate(reversed(self.others))
+        ]
+        found.append(
+            self.copy(
+                self.outgoing, mine, 15, self.partner_receives.at[mine // 2], plane.partner()
+            )
+        )
+        return found
+
+    def passed_copies(self):
+        plane = self.plane
+        slots = [plane.slot(*place) for place in self.others]
+        return [
+            (
+                self.copy(self.outgoing, slot, 0, self.receives.at[slot // 2], plane.partner()),
+                self.copy(
+                    self.gathered.at[slot], slot, 16 + at,
+                    self.partner_receives.at[slot // 2], plane.partner(),
+                ),
+            )
+            for at, slot in enumerate(slots)
+        ]
+
+    def offer(self, last_rows, gain, positive):
+        rows = jnp.concatenate([last_rows[2 * self.pair], last_rows[2 * self.pair + 1]], axis=0)
+        inverse = lax.rsqrt(jnp.mean(rows * rows, axis=-1, keepdims=True) + norm_eps)
+        pooled = rows * inverse * gain
+        embedding = pooled * lax.rsqrt(jnp.sum(pooled * pooled, axis=-1, keepdims=True))
+        pieces = [
+            embedding[m : m + 1, 512 * k : 512 * (k + 1)] for m in range(2) for k in range(7)
+        ]
+        spot = lanes_of((2, 512))
+        pieces.append(jnp.where(spot >= 0, positive[self.pair], 0).astype(F32))
+        packed = jnp.concatenate(pieces, axis=0).astype(BF16)
+        self.outgoing[...] = packed
+        self.gathered[self.plane.slot(0, 0)] = packed
+        for copy in self.own_copies():
+            copy.start()
+
+    def pass_on(self):
+        for arriving, passing in self.passed_copies():
+            arriving.wait_recv()
+            passing.start()
+
+    def from_partner(self):
+        for at in range(16):
+            slot = self.plane.partner_slot(at // 4, at % 4)
+            self.copy(
+                self.outgoing, slot, 0, self.partner_receives.at[at], self.plane.partner()
+            ).wait_recv()
+
+    def drain(self):
+        for copy in self.own_copies():
+            copy.wait_send()
+        for _, passing in self.passed_copies():
+            passing.wait_send()
+
+
+def contrast(plane, exchanges, last_rows, gain, last_grad):
+    at = lax.broadcasted_iota(jnp.int32, (480, 512), 0)
+    chosen = jnp.where(
+        lanes_of((480, 512)) == (at & 31) * 16 + (at >> 5), 1.0, 0.0
+    ).astype(BF16)
+    for exchange in exchanges:
+        exchange.pass_on()
+    for exchange in exchanges:
+        exchange.from_partner()
+    questions, passages, targets = [], [], []
+    for exchange in exchanges:
+        flat = jnp.concatenate([exchange.gathered[i] for i in range(32)], axis=0)
+        found = nn(chosen, flat)
+        pieces = [found[32 * k : 32 * (k + 1)] for k in range(15)]
+        questions.append(jnp.concatenate(pieces[:7], axis=1))
+        passages.append(jnp.concatenate(pieces[7:14], axis=1))
+        targets.append(pieces[14][:, :64])
+    everyone = jnp.concatenate(questions + passages, axis=0).astype(BF16)
+    target = jnp.concatenate(targets, axis=0)
     rows = jnp.concatenate([last_rows[m] for m in range(4)], axis=0)
-    gain = final_gain[...].reshape(1, -1)
     inverse = lax.rsqrt(jnp.mean(rows * rows, axis=-1, keepdims=True) + norm_eps)
     pooled = rows * inverse * gain
     scale = lax.rsqrt(jnp.sum(pooled * pooled, axis=-1, keepdims=True))
-    embedding = pooled * scale
-    spot = lax.broadcasted_iota(jnp.int32, (4, 128), 0)
-    tail = jnp.where(spot < 2, positive[0], positive[1]).astype(F32)
-    packed = jnp.concatenate(
-        [
-            jnp.concatenate([embedding[:, 896 * k : 896 * (k + 1)], tail], axis=1)
-            for k in range(4)
-        ],
-        axis=0,
-    ).astype(BF16)
-    outgoing[...] = packed
-    mine = plane.slot(0, 0)
-    gathered[mine] = packed
-    started = []
-
-    def send(source, slot, receive, place):
-        copy = remote(source, gathered.at[slot], sends.at[len(started)], receive, place)
-        copy.start()
-        started.append(copy)
-
-    others = [(a, b) for a in range(4) for b in range(4) if a or b]
-    others.sort(key=lambda ab: min(ab[0], 4 - ab[0]) + min(ab[1], 4 - ab[1]))
-    for a, b in reversed(others):
-        send(outgoing, mine, receives.at[mine // 2], plane.device(a, b))
-    send(outgoing, mine, partner_receives.at[mine // 2], plane.partner())
-    at = lax.broadcasted_iota(jnp.int32, (128, 512), 0)
-    lane = lanes_of((128, 512))
-    number = at & 63
-    row = (number >> 1) * 16 + (number & 1) * 2 + (at >> 6)
-    selections = [jnp.where(lane == row + 4 * k, 1.0, 0.0).astype(BF16) for k in range(4)]
-    for a, b in others:
-        slot = plane.slot(a, b)
-        remote(
-            outgoing, gathered.at[slot], sends.at[0], receives.at[slot // 2], plane.partner()
-        ).wait_recv()
-        send(gathered.at[slot], slot, partner_receives.at[slot // 2], plane.partner())
-    for at in range(16):
-        slot = plane.partner_slot(at // 4, at % 4)
-        remote(
-            outgoing, gathered.at[slot], sends.at[0], partner_receives.at[at], plane.partner()
-        ).wait_recv()
-    flat = jnp.concatenate([gathered[i] for i in range(32)], axis=0)
-    pieces = [nn(chosen, flat) for chosen in selections]
-    everyone = jnp.concatenate([p[:, :896] for p in pieces], axis=1).astype(BF16)
-    target = pieces[0][:64, 896:960]
     logits = nt(everyone[:64], everyone[64:]) * (1.0 / sharpness_divisor)
     weights = jnp.exp(logits)
     odds = weights / jnp.sum(weights, axis=-1, keepdims=True)
     column = lanes_of((64, 64))
-    hit = jnp.where(target == column.astype(F32), 1.0, 0.0)
+    number = (column & 31) * 2 + (column >> 5)
+    hit = jnp.where(target == number.astype(F32), 1.0, 0.0)
     coefficient = (odds - hit) * (objective_coefficient / sharpness_divisor)
     turned_coefficient = coefficient.T
     line = lax.broadcasted_iota(jnp.int32, (64, 64), 0)
     blank = jnp.zeros((1, 64), F32)
-    replica = mine
+    replica = plane.slot(0, 0)
     chosen_rows = []
     for m in range(4):
         source = turned_coefficient if m % 2 else coefficient
         one = jnp.sum(
-            jnp.where(line == replica * 2 + m // 2, source, 0.0), axis=0, keepdims=True
+            jnp.where(line == replica + 32 * (m // 2), source, 0.0), axis=0, keepdims=True
         )
         chosen_rows.append(jnp.concatenate([one, blank] if m % 2 else [blank, one], axis=1))
     exact = jnp.concatenate(chosen_rows, axis=0)
@@ -413,8 +460,8 @@
     )
     for m in range(4):
         last_grad[m] = row_grad[m : m + 1]
-    for copy in started:
-        copy.wait_send()
+    for exchange in exchanges:
+        exchange.drain()
 
 
 def step_kernel(
@@ -507,6 +554,11 @@
                 turn, inc=1, device_id=plane.partner(), device_id_type=pl.DeviceIdType.MESH
             )
 
+    exchanges = [
+        Exchange(plane, pair, embeds, embed_own, e_send, e_recv, e_cross) for pair in range(2)
+    ]
+    pool_gain = final_gain[...].reshape(1, -1)
+
     def forward(m, carry):
         length = lengths[m]
 
@@ -542,6 +594,11 @@
         saved[m] = kept
         prob[m] = probabilities
         give_turn(me < count - 1, f_turn, m, hop)
+
+        @pl.when(jnp.logical_and(me == count - 1, m == 1))
+        def _():
+            exchanges[0].offer(last_rows, pool_gain, positive)
+
         return carry
 
     lax.fori_loop(0, micros, forward, 0)
@@ -554,8 +611,8 @@
 
     @pl.when(me == count - 1)
     def _():
-        contrast(plane, last_rows, final_gain, positive, embeds, embed_own, e_send, e_recv,
-                 e_cross, last_grad)
+        exchanges[1].offer(last_rows, pool_gain, positive)
+        contrast(plane, exchanges, last_rows, pool_gain, last_grad)
 
     def backward(m, carry):
         length = lengths[m]
@@ -669,13 +726,13 @@
             pltpu.VMEM((seqs, length, 1), F32),
             pltpu.VMEM((seqs, 1, width), F32),
             pltpu.VMEM((seqs, 1, width), F32),
-            pltpu.VMEM((32, 16, 1024), BF16),
-            pltpu.VMEM((16, 1024), BF16),
+            pltpu.VMEM((2, 32, 16, 512), BF16),
+            pltpu.VMEM((2, 16, 512), BF16),
             pltpu.VMEM(block, BF16),
             pltpu.VMEM(block, BF16),
             dma((GATHER_SENDS,)), dma((16, 2)), dma((16,)),
             dma((GATHER_SENDS,)), dma((16, 2)), dma((16,)),
-            dma((31,)), dma((16,)), dma((16,)),
+            dma((2, 31)), dma((2, 16)), dma((2, 16)),
             dma((seqs, chunks)), dma((seqs, chunks)),
             dma((seqs, back_chunks)), dma((seqs, back_chunks)),
             pltpu.SemaphoreType.REGULAR, pltpu.SemaphoreType.REGULAR, dma,

time: 254 us -> 253 us (level)
  no operation moved by 1% of the time
where the time goes in v8:
time: 253 us
  Pallas kernels  253 us (100%)
    pallas_call x1, Pallas kernels, per_device(): pl.pallas_call(step_kernel, out_shape=jax.ShapeDtypeStruct(block, BF16),...  251 us

profile of v8, /device:TPU:1, one launch (start us, length us, event | category | flops | bytes accessed | tf_op | source)
XLA Modules:
  0.0 253.3 jit_solution(8842551238173239297)
XLA Ops:
  0.0 251.2 %shard_map.91.source = bf16[4,48,3584]{2,1,0:T(8,128)(2,1)} custom-call(s32[4]{0:T(128)} %lengths.1, s32[2]{0:T(128)} %positive.1, bf16[4,48,3584]{2,1,0:T(8,128)(2,1)} %bitcast.4, f32[1,3584]{1,0:T(1,128)} %gain.1, bf16[112,1152]{1,0:T(8,128)(2,1)} %bitcast.5, bf16[28,3584]{1,0:T(8,128)(2,1)} %bitcast.6, f32[48,128]{1,0:T(8,128)} %constant.4.clone.cosine, ...), custom_call_target="tpu_custom_call" | custom-call | tf_op jit(solution)/shard_map/pallas_call | solution.py:712
  251.2 2.1 shard_map.92

commit v9 on v7

--- a/solution.py
+++ b/solution.py
@@ -19,6 +19,7 @@
 
 LENGTH = 48
 EARLY = 2
+BACK_EARLY = 1
 PAIRS = 7
 F32 = jnp.float32
 BF16 = jnp.bfloat16
@@ -495,10 +496,10 @@
         def _():
             pl.semaphore_wait(turn, 1)
 
-    def give_turn(sending, turn, m, copies):
+    def give_turn(sending, turn, m, copies, early):
         @pl.when(sending)
         def _():
-            for k in range(EARLY):
+            for k in range(early):
                 copies(m, k).wait_send()
 
         @pl.when(jnp.logical_and(sending, m + plane.core < micros))
@@ -541,7 +542,7 @@
             )
         saved[m] = kept
         prob[m] = probabilities
-        give_turn(me < count - 1, f_turn, m, hop)
+        give_turn(me < count - 1, f_turn, m, hop, EARLY)
         return carry
 
     lax.fori_loop(0, micros, forward, 0)
@@ -594,7 +595,7 @@
             def _():
                 back_hop(m, k).start()
 
-        give_turn(me > 0, b_turn, m, back_hop)
+        give_turn(me > 0, b_turn, m, back_hop, BACK_EARLY)
         return carry
 
     lax.fori_loop(0, micros, backward, 0)
@@ -602,7 +603,7 @@
     @pl.when(me > 0)
     def _():
         for m in range(micros):
-            for k in range(EARLY, len(BACK_CHUNKS)):
+            for k in range(BACK_EARLY, len(BACK_CHUNKS)):
                 back_hop(m, k).wait_send()
 
 

time: 254 us -> 257 us (1.012)
  no operation moved by 1% of the time
where the time goes in v9:
time: 257 us; the launch traced here: 256 us
  Pallas kernels  256 us (100%)
    pallas_call x1, Pallas kernels, per_device(): pl.pallas_call(step_kernel, out_shape=jax.ShapeDtypeStruct(block, BF16),...  254 us

profile of v9, /device:TPU:1, one launch (start us, length us, event | category | flops | bytes accessed | tf_op | source)
XLA Modules:
  0.0 256.4 jit_solution(11990993176001030981)
XLA Ops:
  0.0 254.3 %shard_map.91.source = bf16[4,48,3584]{2,1,0:T(8,128)(2,1)} custom-call(s32[4]{0:T(128)} %lengths.1, s32[2]{0:T(128)} %positive.1, bf16[4,48,3584]{2,1,0:T(8,128)(2,1)} %bitcast.4, f32[1,3584]{1,0:T(1,128)} %gain.1, bf16[112,1152]{1,0:T(8,128)(2,1)} %bitcast.5, bf16[28,3584]{1,0:T(8,128)(2,1)} %bitcast.6, f32[48,128]{1,0:T(8,128)} %constant.4.clone.cosine, ...), custom_call_target="tpu_custom_call" | custom-call | tf_op jit(solution)/shard_map/pallas_call | solution.py:656
  254.3 2.1 shard_map.92
